TPU v7x, 256 devices: a whole 4x4x8 slice. The times are simulated.
256 devices in a mesh: tok: 64 (over y, z, core), feat: 4 (over x).
Axes of the slice: x: 4, y: 4, z: 8, core: 2. Of those that a mesh axis runs over, the one named last changes fastest.
Arguments:
- first_acts: bfloat16 [81920, 3584], P('tok', 'feat'), may hold values from -6 to 6
- second_acts: bfloat16 [81920, 3584], P('tok', 'feat'), may hold values from -6 to 6
- start_dirs: bfloat16 [3584, 256], P('feat'), may hold values from -0.09375 to 0.09375
Outputs:
- first_dirs: bfloat16 [3584, 256], P('feat')
- second_dirs: bfloat16 [3584, 256], P('feat')
- correlation: float32 [256, 256], replicated
All inputs are finite; a program needn't handle non-finite values.
Results may differ from a plain program's by a relative error of at most 0.006.
Values may be sent and summed in bfloat16 or wider, within the bound.
A program may use at most 128 MiB of HBM per device.

v0:
```python
import jax
import jax.numpy as jnp
from jax import lax
from jax.sharding import Mesh
from jax.sharding import PartitionSpec as P

D = 3584
ITERS = 2
TOK = ("tok_0", "tok_1", "tok_2")


def padded_to(lines, size):
    spare = -lines.shape[0] % size
    if not spare:
        return lines
    return jnp.concatenate([lines, jnp.zeros((spare, *lines.shape[1:]), lines.dtype)])


def copy_for_each(shard, axis):
    copies = jnp.broadcast_to(shard, (lax.axis_size(axis), *shard.shape))
    return lax.all_to_all(copies, axis, split_axis=0, concat_axis=0, tiled=True)


def joined_along(blocks, dim):
    blocks = jnp.moveaxis(blocks, 0, dim)
    lengths = blocks.shape
    return blocks.reshape(*lengths[:dim], lengths[dim] * lengths[dim + 1], *lengths[dim + 2 :])


def gathered_copies(shard, axis, dim):
    blocks = copy_for_each(shard, axis)
    return joined_along(blocks, dim)


def split_up(shard, dim, size):
    lengths = shard.shape
    blocks = shard.reshape(*lengths[:dim], size, lengths[dim] // size, *lengths[dim + 1 :])
    return jnp.moveaxis(blocks, dim, 0)


def summed_on_arrival(shard, axis, dim):
    blocks = split_up(shard, dim, lax.axis_size(axis))
    arrived = lax.all_to_all(blocks, axis, split_axis=0, concat_axis=0, tiled=True)
    return arrived.sum(axis=0)


def sum_by_parts(shard, axes):
    lines = shard.reshape(-1, shard.shape[-1])
    padded = padded_to(lines, lax.axis_size(axes))
    whole = gathered_copies(summed_on_arrival(padded, axes, 0), axes, 0)
    return lax.slice_in_dim(whole, 0, len(lines)).reshape(shard.shape)


def sum_in_two_steps(shard, axes, dim):
    far, near = axes
    blocks = split_up(shard, dim, lax.axis_size(far))
    nearer = summed_on_arrival(blocks, near, dim + 1)
    arrived = lax.all_to_all(nearer, far, split_axis=0, concat_axis=0, tiled=True)
    return arrived.sum(axis=0)


def gather_axes(shard, axes, dim):
    far, near = axes
    blocks = copy_for_each(copy_for_each(shard, far), near)
    return joined_along(blocks.swapaxes(0, 1).reshape(-1, *shard.shape), dim)


def sum_by_parts_2(shard, axes):
    lines = shard.reshape(-1, shard.shape[-1])
    own = sum_in_two_steps(
        padded_to(lines, lax.axis_size(axes[0]) * lax.axis_size(axes[1])), axes, 0
    )
    whole = gather_axes(own, axes, 0)
    return whole[: len(lines)].reshape(shard.shape)


def over_copies(shard, axis):
    everything = copy_for_each(shard, axis)
    return jnp.sum(everything, axis=0)


def in_one(arrays, axis):
    ravelled, at, gathered = (jnp.concatenate([a.reshape(-1) for a in arrays]), 0, [])
    so_far = over_copies(ravelled, axis)
    for a in arrays:
        gathered.append(so_far[at : at + a.size].reshape(a.shape))
        at += a.size
    return tuple(gathered)


def project(source, dirs):
    partial_value = jnp.dot(source, dirs, preferred_element_type=jnp.float32)
    z_rows = lax.psum(partial_value, "feat").astype(jnp.bfloat16)
    return (z_rows, z_rows, 0)


def total(pieces):
    return jax.tree.map(lambda part: sum_by_parts(part, TOK), pieces)


def half_step(source, target, dirs, scale, tokens):
    z_rows, share, offset = project(source, dirs)
    sums = total((jnp.dot(share.T, share, preferred_element_type=jnp.float32),))
    lower = jnp.linalg.cholesky(sums[0] / tokens)
    term = jnp.einsum("tf,tk->fk", target, z_rows, preferred_element_type=jnp.float32)
    cross = sum_by_parts_2(term, (("tok_0", "tok_1"), "tok_2")) / tokens
    solved = lax.linalg.triangular_solve(
        lower, cross, left_side=False, lower=True, transpose_a=True
    )
    new_dirs = (solved * scale[:, None]).astype(jnp.bfloat16)
    return (new_dirs, z_rows, lower)


def body(first_acts, second_acts, start_dirs):
    tokens = first_acts.shape[0] * lax.axis_size(TOK)
    sq_first = jnp.sum(jnp.square(first_acts.astype(jnp.float32)), axis=0)
    sq_second = jnp.sum(jnp.square(second_acts.astype(jnp.float32)), axis=0)
    sum_first, sum_second = in_one((sq_first, sq_second), TOK)
    root = jnp.sqrt(jnp.float32(D))
    scale_first = root / (sum_first / tokens + 0.5)
    scale_second = root / (sum_second / tokens + 0.5)
    second = start_dirs
    for step in range(ITERS):
        first, z_second, lower_second = half_step(
            second_acts, first_acts, second, scale_first, tokens
        )
        second, z_first, lower_first = half_step(
            first_acts, second_acts, first, scale_second, tokens
        )
    z_last, share, offset = project(second_acts, second)
    gram_last, pair = total(
        (
            jnp.dot(share.T, share, preferred_element_type=jnp.float32),
            jnp.dot(z_first.T, share, preferred_element_type=jnp.float32),
        )
    )
    lower_last = jnp.linalg.cholesky(gram_last / tokens)
    left = lax.linalg.triangular_solve(lower_first, pair / tokens, left_side=True, lower=True)
    correlation = lax.linalg.triangular_solve(
        lower_last, left, left_side=False, lower=True, transpose_a=True
    )
    return (first, second, correlation)


def solution(mesh):
    split = Mesh(
        mesh.devices.reshape(4, 8, 2, mesh.shape["feat"]), ("tok_0", "tok_1", "tok_2", "feat")
    )
    in_specs = (P(TOK, "feat"), P(TOK, "feat"), P("feat", None))
    out_specs = (P("feat", None), P("feat", None), P())
    return jax.shard_map(body, mesh=split, in_specs=in_specs, out_specs=out_specs, check_vma=False)
```

profile of v0, /device:TPU:1, one launch (start us, length us, event | category | flops | bytes accessed | tf_op | source)
XLA Modules:
  0.0 990.4 jit_solution(7535175842403407701)
XLA Ops:
  4.2 30.1 %all-reduce.6 = bf16[1280,256]{1,0:T(8,128)(2,1)S(1)} all-reduce(f32[1280,256]{1,0:T(8,128)S(1)} %fusion.90), channel_id=1, replica_groups=mesh['tok_0'=4,'tok_1'=8,'tok_2'=2,'feat'=4] {'feat'}, use_global_device_ids=true, to_apply=%region_0.0 | all-reduce | flops 327680 | bytes 1966080 | tf_op jit(solution)/shard_map/psum | solution.py:93
  38.9 9.7 all-to-all-start.2
  50.2 11.3 %all-to-all-start = ((f32[64,4,256]{2,1,0:T(4,128)}), f32[64,4,256]{2,1,0:T(4,128)S(1)}, u32[]{:S(2)}, u32[]{:S(2)}) async-start(f32[64,4,256]{2,1,0:T(4,128)} %reshape.83), calls=%async_computation | async-start | bytes 524288 | tf_op jit(solution)/shard_map/all_to_all | solution.py:43
  64.5 9.0 all-to-all-done
  80.7 12.0 %all-to-all-done.3 = f32[32,14,256]{2,1,0:T(8,128)S(1)} async-done(((f32[32,14,256]{2,1,0:T(8,128)}), f32[32,14,256]{2,1,0:T(8,128)S(1)}, u32[]{:S(2)}, u32[]{:S(2)}) %all-to-all-start.3) | async-done | bytes 458784 | tf_op jit(solution)/shard_map/all_to_all | solution.py:58
  93.8 9.4 all-to-all-start.6
  103.3 15.8 %all-to-all-done.6 = f32[64,1,1792]{2,1,0:T(1,128)S(1)} async-done(((f32[64,1,1792]{2,1,0:T(1,128)}), f32[64,1,1792]{2,1,0:T(1,128)S(1)}, u32[]{:S(2)}, u32[]{:S(2)}) %all-to-all-start.6) | async-done | bytes 458784 | tf_op jit(solution)/shard_map/all_to_all | solution.py:21
  119.8 6.3 all-to-all-start.1
  127.5 10.5 %all-to-all-done.1 = f32[64,4,256]{2,1,0:T(4,128)S(1)} async-done(((f32[64,4,256]{2,1,0:T(4,128)}), f32[64,4,256]{2,1,0:T(4,128)S(1)}, u32[]{:S(2)}, u32[]{:S(2)}) %all-to-all-start.1) | async-done | bytes 262176 | tf_op jit(solution)/shard_map/all_to_all | solution.py:21
  138.9 5.2 all-to-all-start.4
  146.8 11.7 %cholesky.256 = f32[128,128]{1,0:T(8,128)S(1)} custom-call(f32[128,128]{1,0:T(8,128)S(1)} %cholesky.422), custom_call_target="Cholesky" | custom-call | tf_op jit(solution)/shard_map/jit(cholesky)/cholesky | solution.py:104
  158.6 9.8 custom-call.26
  170.6 11.7 %cholesky.273 = f32[128,128]{1,0:T(8,128)S(1)} custom-call(f32[128,128]{1,0:T(8,128)S(1)} %convolution_subtract_fusion.10), custom_call_target="Cholesky" | custom-call | tf_op jit(solution)/shard_map/jit(cholesky)/cholesky | solution.py:104
  188.3 19.9 %custom-call.27 = f32[2,128,128]{1,2,0:T(8,128)S(1)} custom-call(f32[2,128,128]{2,1,0:T(8,128)S(1)} %get-tuple-element.47), custom_call_target="InvertDiagBlocksLowerTriangular" | custom-call | tf_op jit(solution)/shard_map/triangular_solve/custom-call.0 | solution.py:107
  221.7 29.3 %all-reduce.7 = bf16[1280,256]{0,1:T(8,128)(2,1)S(1)} all-reduce(f32[1280,256]{0,1:T(8,128)} %convolution_bitcast_fusion.3), channel_id=1, replica_groups=mesh['tok_0'=4,'tok_1'=8,'tok_2'=2,'feat'=4] {'feat'}, use_global_device_ids=true, to_apply=%region_11.14 | all-reduce | flops 327680 | bytes 1966080 | tf_op jit(solution)/shard_map/psum | solution.py:93
  258.2 8.5 all_to_all.147
  266.7 10.4 %all-to-all-start.7 = ((f32[64,4,256]{2,1,0:T(4,128)}), f32[64,4,256]{2,1,0:T(4,128)S(1)}, u32[]{:S(2)}, u32[]{:S(2)}) async-start(f32[64,4,256]{2,1,0:T(4,128)} %reshape.84), calls=%async_computation.7 | async-start | bytes 524288 | tf_op jit(solution)/shard_map/all_to_all | solution.py:43
  280.1 9.0 all-to-all-done.7
  294.2 14.1 %all-to-all-done.10 = f32[32,14,256]{2,1,0:T(8,128)S(1)} async-done(((f32[32,14,256]{2,1,0:T(8,128)}), f32[32,14,256]{2,1,0:T(8,128)S(1)}, u32[]{:S(2)}, u32[]{:S(2)}) %all-to-all-start.10) | async-done | bytes 458784 | tf_op jit(solution)/shard_map/all_to_all | solution.py:58
  309.1 9.4 all-to-all-start.8
  318.6 11.9 %all-to-all-done.8 = f32[64,4,256]{2,1,0:T(4,128)S(1)} async-done(((f32[64,4,256]{2,1,0:T(4,128)}), f32[64,4,256]{2,1,0:T(4,128)S(1)}, u32[]{:S(2)}, u32[]{:S(2)}) %all-to-all-start.8) | async-done | bytes 262176 | tf_op jit(solution)/shard_map/all_to_all | solution.py:21
  331.3 5.4 all-to-all-start.11
  339.5 11.7 %cholesky.290 = f32[128,128]{1,0:T(8,128)S(1)} custom-call(f32[128,128]{1,0:T(8,128)S(1)} %cholesky.425), custom_call_target="Cholesky" | custom-call | tf_op jit(solution)/shard_map/jit(cholesky)/cholesky | solution.py:104
  351.2 9.8 custom-call.28
  363.2 11.7 %cholesky.307 = f32[128,128]{1,0:T(8,128)S(1)} custom-call(f32[128,128]{1,0:T(8,128)S(1)} %convolution_subtract_fusion.9), custom_call_target="Cholesky" | custom-call | tf_op jit(solution)/shard_map/jit(cholesky)/cholesky | solution.py:104
  381.9 19.8 %custom-call.29 = f32[2,128,128]{1,2,0:T(8,128)S(1)} custom-call(f32[2,128,128]{2,1,0:T(8,128)S(1)} %get-tuple-element.48), custom_call_target="InvertDiagBlocksLowerTriangular" | custom-call | tf_op jit(solution)/shard_map/triangular_solve/custom-call.0 | solution.py:107
  415.0 29.2 %all-reduce.8 = bf16[1280,256]{0,1:T(8,128)(2,1)S(1)} all-reduce(f32[1280,256]{0,1:T(8,128)} %convolution_bitcast_fusion.2), channel_id=1, replica_groups=mesh['tok_0'=4,'tok_1'=8,'tok_2'=2,'feat'=4] {'feat'}, use_global_device_ids=true, to_apply=%region_15.18 | all-reduce | flops 327680 | bytes 1966080 | tf_op jit(solution)/shard_map/psum | solution.py:93
  453.1 9.7 all_to_all.149
  462.8 9.9 %all-to-all-start.13 = ((f32[64,4,256]{2,1,0:T(4,128)}), f32[64,4,256]{2,1,0:T(4,128)S(1)}, u32[]{:S(2)}, u32[]{:S(2)}) async-start(f32[64,4,256]{2,1,0:T(4,128)} %reshape.85), calls=%async_computation.13 | async-start | bytes 524288 | tf_op jit(solution)/shard_map/all_to_all | solution.py:43
  475.6 9.0 all-to-all-done.13
  489.8 14.1 %all-to-all-done.16 = f32[32,14,256]{2,1,0:T(8,128)S(1)} async-done(((f32[32,14,256]{2,1,0:T(8,128)}), f32[32,14,256]{2,1,0:T(8,128)S(1)}, u32[]{:S(2)}, u32[]{:S(2)}) %all-to-all-start.16) | async-done | bytes 458784 | tf_op jit(solution)/shard_map/all_to_all | solution.py:58
  504.6 9.4 all-to-all-start.14
  514.1 11.9 %all-to-all-done.14 = f32[64,4,256]{2,1,0:T(4,128)S(1)} async-done(((f32[64,4,256]{2,1,0:T(4,128)}), f32[64,4,256]{2,1,0:T(4,128)S(1)}, u32[]{:S(2)}, u32[]{:S(2)}) %all-to-all-start.14) | async-done | bytes 262176 | tf_op jit(solution)/shard_map/all_to_all | solution.py:21
  526.8 5.2 all-to-all-start.17
  534.8 11.7 %cholesky.324 = f32[128,128]{1,0:T(8,128)S(1)} custom-call(f32[128,128]{1,0:T(8,128)S(1)} %cholesky.428), custom_call_target="Cholesky" | custom-call | tf_op jit(solution)/shard_map/jit(cholesky)/cholesky | solution.py:104
  546.6 9.8 custom-call.30
  558.6 11.7 %cholesky.341 = f32[128,128]{1,0:T(8,128)S(1)} custom-call(f32[128,128]{1,0:T(8,128)S(1)} %convolution_subtract_fusion.8), custom_call_target="Cholesky" | custom-call | tf_op jit(solution)/shard_map/jit(cholesky)/cholesky | solution.py:104
  577.0 20.1 %custom-call.31 = f32[2,128,128]{1,2,0:T(8,128)S(1)} custom-call(f32[2,128,128]{2,1,0:T(8,128)S(1)} %get-tuple-element.49), custom_call_target="InvertDiagBlocksLowerTriangular" | custom-call | tf_op jit(solution)/shard_map/triangular_solve/custom-call.0 | solution.py:107
  610.5 29.3 %all-reduce.9 = bf16[1280,256]{0,1:T(8,128)(2,1)S(1)} all-reduce(f32[1280,256]{0,1:T(8,128)} %convolution_bitcast_fusion.1), channel_id=1, replica_groups=mesh['tok_0'=4,'tok_1'=8,'tok_2'=2,'feat'=4] {'feat'}, use_global_device_ids=true, to_apply=%region_19.22 | all-reduce | flops 327680 | bytes 1966080 | tf_op jit(solution)/shard_map/psum | solution.py:93
  650.9 9.3 all_to_all.151
  660.2 10.6 %all-to-all-start.19 = ((f32[64,4,256]{2,1,0:T(4,128)}), f32[64,4,256]{2,1,0:T(4,128)}, u32[]{:S(2)}, u32[]{:S(2)}) async-start(f32[64,4,256]{2,1,0:T(4,128)} %reshape.86), calls=%async_computation.19 | async-start | bytes 524288 | tf_op jit(solution)/shard_map/all_to_all | solution.py:43
  675.0 7.7 all-to-all-done.19
  682.7 5.2 all-to-all-start.22
  688.9 13.2 %all-to-all-done.22 = f32[32,14,256]{2,1,0:T(8,128)} async-done(((f32[32,14,256]{2,1,0:T(8,128)}), f32[32,14,256]{2,1,0:T(8,128)}, u32[]{:S(2)}, u32[]{:S(2)}) %all-to-all-start.22) | async-done | bytes 458784 | tf_op jit(solution)/shard_map/all_to_all | solution.py:58
  702.8 9.6 all-to-all-start.20
  713.5 10.8 %all-to-all-done.20 = f32[64,4,256]{2,1,0:T(4,128)} async-done(((f32[64,4,256]{2,1,0:T(4,128)}), f32[64,4,256]{2,1,0:T(4,128)}, u32[]{:S(2)}, u32[]{:S(2)}) %all-to-all-start.20) | async-done | bytes 262176 | tf_op jit(solution)/shard_map/all_to_all | solution.py:21
  725.1 5.3 all-to-all-start.23
  737.5 11.7 %cholesky.358 = f32[128,128]{1,0:T(8,128)S(1)} custom-call(f32[128,128]{1,0:T(8,128)S(1)} %cholesky.431), custom_call_target="Cholesky" | custom-call | tf_op jit(solution)/shard_map/jit(cholesky)/cholesky | solution.py:104
  750.0 9.8 custom-call.32
  762.6 11.7 %cholesky.375 = f32[128,128]{1,0:T(8,128)S(1)} custom-call(f32[128,128]{1,0:T(8,128)S(1)} %convolution_subtract_fusion.7), custom_call_target="Cholesky" | custom-call | tf_op jit(solution)/shard_map/jit(cholesky)/cholesky | solution.py:104
  779.3 5.9 while.14
  785.8 20.7 %custom-call.33 = f32[2,128,128]{1,2,0:T(8,128)S(1)} custom-call(f32[2,128,128]{2,1,0:T(8,128)} %copy-done.17), custom_call_target="InvertDiagBlocksLowerTriangular" | custom-call | tf_op jit(solution)/shard_map/triangular_solve/custom-call.0 | solution.py:107
  823.9 29.2 %all-reduce.10 = bf16[1280,256]{0,1:T(8,128)(2,1)S(1)} all-reduce(f32[1280,256]{0,1:T(8,128)} %convolution_bitcast_fusion), channel_id=1, replica_groups=mesh['tok_0'=4,'tok_1'=8,'tok_2'=2,'feat'=4] {'feat'}, use_global_device_ids=true, to_apply=%region_23.26 | all-reduce | flops 327680 | bytes 1966080 | tf_op jit(solution)/shard_map/psum | solution.py:93
  854.3 15.3 %all-to-all-start.27 = ((f32[64,4,256]{2,1,0:T(4,128)}), f32[64,4,256]{2,1,0:T(4,128)S(1)}, u32[]{:S(2)}, u32[]{:S(2)}) async-start(f32[64,4,256]{2,1,0:T(4,128)} %reshape.88), calls=%async_computation.27 | async-start | bytes 524288 | tf_op jit(solution)/shard_map/all_to_all | solution.py:43
  870.7 10.8 %all-to-all-done.27 = f32[64,4,256]{2,1,0:T(4,128)S(1)} async-done(((f32[64,4,256]{2,1,0:T(4,128)}), f32[64,4,256]{2,1,0:T(4,128)S(1)}, u32[]{:S(2)}, u32[]{:S(2)}) %all-to-all-start.27) | async-done | bytes 262176 | tf_op jit(solution)/shard_map/all_to_all | solution.py:43
  881.5 6.0 all-to-all-start.25
  887.6 11.9 %all-to-all-done.25 = f32[64,4,256]{2,1,0:T(4,128)S(1)} async-done(((f32[64,4,256]{2,1,0:T(4,128)}), f32[64,4,256]{2,1,0:T(4,128)S(1)}, u32[]{:S(2)}, u32[]{:S(2)}) %all-to-all-start.25) | async-done | bytes 262176 | tf_op jit(solution)/shard_map/all_to_all | solution.py:43
  900.2 6.0 all-to-all-start.28
  908.3 9.9 %all-to-all-done.28 = f32[64,4,256]{2,1,0:T(4,128)S(1)} async-done(((f32[64,4,256]{2,1,0:T(4,128)}), f32[64,4,256]{2,1,0:T(4,128)S(1)}, u32[]{:S(2)}, u32[]{:S(2)}) %all-to-all-start.28) | async-done | bytes 262176 | tf_op jit(solution)/shard_map/all_to_all | solution.py:21
  919.0 6.6 all-to-all-start.26
  925.9 11.7 %cholesky.392 = f32[128,128]{1,0:T(8,128)S(1)} custom-call(f32[128,128]{1,0:T(8,128)S(1)} %cholesky.434), custom_call_target="Cholesky" | custom-call | tf_op jit(solution)/shard_map/jit(cholesky)/cholesky | solution.py:137
  937.7 9.8 custom-call.34
  948.0 11.7 %cholesky.409 = f32[128,128]{1,0:T(8,128)S(1)} custom-call(f32[128,128]{1,0:T(8,128)S(1)} %convolution_subtract_fusion.6), custom_call_target="Cholesky" | custom-call | tf_op jit(solution)/shard_map/jit(cholesky)/cholesky | solution.py:137
  966.4 19.8 %custom-call.18 = f32[2,128,128]{1,2,0:T(8,128)S(1)} custom-call(f32[2,128,128]{2,1,0:T(8,128)S(1)} %get-tuple-element.28), custom_call_target="InvertDiagBlocksLowerTriangular" | custom-call | tf_op jit(solution)/shard_map/triangular_solve | solution.py:139
  (275 shorter events, 218.4 us)
Async XLA Ops:
  0.6 1.0 copy-start
  34.2 3.1 copy-start.15
  37.4 11.1 %copy-start.16 = (bf16[1280,256]{1,0:T(8,128)(2,1)S(1)}, bf16[1280,256]{1,0:T(8,128)(2,1)}, u32[]{:S(2)}) copy-start(bf16[1280,256]{1,0:T(8,128)(2,1)} %copy-done.15) | copy-start | bytes 1966084
  38.9 11.3 %all-to-all-start.2 = ((f32[2,32,14,256]{3,1,2,0:T(8,128)}), f32[2,32,14,256]{3,1,2,0:T(8,128)S(1)}, u32[]{:S(2)}, u32[]{:S(2)}) async-start(f32[2,32,14,256]{3,1,2,0:T(8,128)} %copy.128), calls=%async_computation.2 | async-start | bytes 1835008 | tf_op jit(solution)/shard_map/all_to_all | solution.py:43
  49.0 29.6 %copy-start.2 = (bf16[1280,896]{1,0:T(8,128)(2,1)S(1)}, bf16[1280,896]{1,0:T(8,128)(2,1)}, u32[]{:S(2)}) copy-start(bf16[1280,896]{1,0:T(8,128)(2,1)} %param.7) | copy-start | bytes 6881284
  50.2 23.3 %all-to-all-start = ((f32[64,4,256]{2,1,0:T(4,128)}), f32[64,4,256]{2,1,0:T(4,128)S(1)}, u32[]{:S(2)}, u32[]{:S(2)}) async-start(f32[64,4,256]{2,1,0:T(4,128)} %reshape.83), calls=%async_computation | async-start | bytes 524288 | tf_op jit(solution)/shard_map/all_to_all | solution.py:43
  73.5 19.3 %all-to-all-start.3 = ((f32[32,14,256]{2,1,0:T(8,128)}), f32[32,14,256]{2,1,0:T(8,128)S(1)}, u32[]{:S(2)}, u32[]{:S(2)}) async-start(f32[32,14,256]{2,1,0:T(8,128)} %copy.129), calls=%async_computation.3 | async-start | bytes 1048576 | tf_op jit(solution)/shard_map/all_to_all | solution.py:58
  78.6 1.6 copy-start.3
  93.8 25.3 %all-to-all-start.6 = ((f32[64,1,1792]{2,1,0:T(1,128)}), f32[64,1,1792]{2,1,0:T(1,128)S(1)}, u32[]{:S(2)}, u32[]{:S(2)}) async-start(f32[64,1,1792]{2,1,0:T(1,128)} %broadcast_in_dim.53), calls=%async_computation.6 | async-start | bytes 917504 | tf_op jit(solution)/shard_map/all_to_all | solution.py:21
  119.8 18.3 %all-to-all-start.1 = ((f32[64,4,256]{2,1,0:T(4,128)}), f32[64,4,256]{2,1,0:T(4,128)S(1)}, u32[]{:S(2)}, u32[]{:S(2)}) async-start(f32[64,4,256]{2,1,0:T(4,128)} %broadcast_in_dim.50), calls=%async_computation.1 | async-start | bytes 524288 | tf_op jit(solution)/shard_map/all_to_all | solution.py:21
  138.9 69.3 %all-to-all-start.4 = ((f32[32,14,256]{2,1,0:T(8,128)}), f32[32,14,256]{2,1,0:T(8,128)S(1)}, u32[]{:S(2)}, u32[]{:S(2)}) async-start(f32[32,14,256]{2,1,0:T(8,128)} %broadcast_in_dim.51), calls=%async_computation.4 | async-start | bytes 1048576 | tf_op jit(solution)/shard_map/all_to_all | solution.py:21
  144.1 40.3 %copy-start.20 = (s32[2]{0:T(128)S(1)}, s32[2]{0:T(128)}, u32[]{:S(2)}) copy-start(s32[2]{0:T(128)} %iota_multiply_fusion) | copy-start | bytes 28
  146.1 0.7 copy-start.11
  188.3 25.2 %copy-start.8 = (f32[256,256]{1,0:T(8,128)}, f32[256,256]{1,0:T(8,128)S(1)}, u32[]{:S(2)}) copy-start(f32[256,256]{1,0:T(8,128)S(1)} %get-tuple-element.398) | copy-start | bytes 786436
  214.2 5.4 copy-start.19
  215.3 4.4 copy-start.4
  266.7 22.4 %all-to-all-start.7 = ((f32[64,4,256]{2,1,0:T(4,128)}), f32[64,4,256]{2,1,0:T(4,128)S(1)}, u32[]{:S(2)}, u32[]{:S(2)}) async-start(f32[64,4,256]{2,1,0:T(4,128)} %reshape.84), calls=%async_computation.7 | async-start | bytes 524288 | tf_op jit(solution)/shard_map/all_to_all | solution.py:43
  289.1 19.3 %all-to-all-start.10 = ((f32[32,14,256]{2,1,0:T(8,128)}), f32[32,14,256]{2,1,0:T(8,128)S(1)}, u32[]{:S(2)}, u32[]{:S(2)}) async-start(f32[32,14,256]{2,1,0:T(8,128)} %copy.136), calls=%async_computation.10 | async-start | bytes 1048576 | tf_op jit(solution)/shard_map/all_to_all | solution.py:58
  309.1 21.4 %all-to-all-start.8 = ((f32[64,4,256]{2,1,0:T(4,128)}), f32[64,4,256]{2,1,0:T(4,128)S(1)}, u32[]{:S(2)}, u32[]{:S(2)}) async-start(f32[64,4,256]{2,1,0:T(4,128)} %broadcast_in_dim.54), calls=%async_computation.8 | async-start | bytes 524288 | tf_op jit(solution)/shard_map/all_to_all | solution.py:21
  331.3 70.4 %all-to-all-start.11 = ((f32[32,14,256]{2,1,0:T(8,128)}), f32[32,14,256]{2,1,0:T(8,128)S(1)}, u32[]{:S(2)}, u32[]{:S(2)}) async-start(f32[32,14,256]{2,1,0:T(8,128)} %broadcast_in_dim.55), calls=%async_computation.11 | async-start | bytes 1048576 | tf_op jit(solution)/shard_map/all_to_all | solution.py:21
  338.8 0.7 copy-start.12
  381.8 25.2 %copy-start.9 = (f32[256,256]{1,0:T(8,128)}, f32[256,256]{1,0:T(8,128)S(1)}, u32[]{:S(2)}) copy-start(f32[256,256]{1,0:T(8,128)S(1)} %get-tuple-element.399) | copy-start | bytes 786436
  407.7 5.3 copy-start.18
  462.8 21.9 %all-to-all-start.13 = ((f32[64,4,256]{2,1,0:T(4,128)}), f32[64,4,256]{2,1,0:T(4,128)S(1)}, u32[]{:S(2)}, u32[]{:S(2)}) async-start(f32[64,4,256]{2,1,0:T(4,128)} %reshape.85), calls=%async_computation.13 | async-start | bytes 524288 | tf_op jit(solution)/shard_map/all_to_all | solution.py:43
  484.6 19.3 %all-to-all-start.16 = ((f32[32,14,256]{2,1,0:T(8,128)}), f32[32,14,256]{2,1,0:T(8,128)S(1)}, u32[]{:S(2)}, u32[]{:S(2)}) async-start(f32[32,14,256]{2,1,0:T(8,128)} %copy.142), calls=%async_computation.16 | async-start | bytes 1048576 | tf_op jit(solution)/shard_map/all_to_all | solution.py:58
  504.6 21.4 %all-to-all-start.14 = ((f32[64,4,256]{2,1,0:T(4,128)}), f32[64,4,256]{2,1,0:T(4,128)S(1)}, u32[]{:S(2)}, u32[]{:S(2)}) async-start(f32[64,4,256]{2,1,0:T(4,128)} %broadcast_in_dim.57), calls=%async_computation.14 | async-start | bytes 524288 | tf_op jit(solution)/shard_map/all_to_all | solution.py:21
  526.8 70.2 %all-to-all-start.17 = ((f32[32,14,256]{2,1,0:T(8,128)}), f32[32,14,256]{2,1,0:T(8,128)S(1)}, u32[]{:S(2)}, u32[]{:S(2)}) async-start(f32[32,14,256]{2,1,0:T(8,128)} %broadcast_in_dim.58), calls=%async_computation.17 | async-start | bytes 1048576 | tf_op jit(solution)/shard_map/all_to_all | solution.py:21
  534.1 0.7 copy-start.13
  577.0 25.4 %copy-start.10 = (f32[256,256]{1,0:T(8,128)}, f32[256,256]{1,0:T(8,128)S(1)}, u32[]{:S(2)}) copy-start(f32[256,256]{1,0:T(8,128)S(1)} %get-tuple-element.400) | copy-start | bytes 786436
  604.1 4.4 copy-start.5
  660.2 22.5 %all-to-all-start.19 = ((f32[64,4,256]{2,1,0:T(4,128)}), f32[64,4,256]{2,1,0:T(4,128)}, u32[]{:S(2)}, u32[]{:S(2)}) async-start(f32[64,4,256]{2,1,0:T(4,128)} %reshape.86), calls=%async_computation.19 | async-start | bytes 524288 | tf_op jit(solution)/shard_map/all_to_all | solution.py:43
  682.7 19.4 %all-to-all-start.22 = ((f32[32,14,256]{2,1,0:T(8,128)}), f32[32,14,256]{2,1,0:T(8,128)}, u32[]{:S(2)}, u32[]{:S(2)}) async-start(f32[32,14,256]{2,1,0:T(8,128)} %copy.148), calls=%async_computation.22 | async-start | bytes 1048576 | tf_op jit(solution)/shard_map/all_to_all | solution.py:58
  702.8 21.5 %all-to-all-start.20 = ((f32[64,4,256]{2,1,0:T(4,128)}), f32[64,4,256]{2,1,0:T(4,128)}, u32[]{:S(2)}, u32[]{:S(2)}) async-start(f32[64,4,256]{2,1,0:T(4,128)} %broadcast_in_dim.60), calls=%async_computation.20 | async-start | bytes 524288 | tf_op jit(solution)/shard_map/all_to_all | solution.py:21
  725.1 81.4 %all-to-all-start.23 = ((f32[32,14,256]{2,1,0:T(8,128)}), f32[32,14,256]{2,1,0:T(8,128)}, u32[]{:S(2)}, u32[]{:S(2)}) async-start(f32[32,14,256]{2,1,0:T(8,128)} %broadcast_in_dim.61), calls=%async_computation.23 | async-start | bytes 1048576 | tf_op jit(solution)/shard_map/all_to_all | solution.py:21
  736.8 0.7 copy-start.14
  785.2 0.7 copy-start.17
  821.1 0.8 copy-start.6
  854.3 27.2 %all-to-all-start.27 = ((f32[64,4,256]{2,1,0:T(4,128)}), f32[64,4,256]{2,1,0:T(4,128)S(1)}, u32[]{:S(2)}, u32[]{:S(2)}) async-start(f32[64,4,256]{2,1,0:T(4,128)} %reshape.88), calls=%async_computation.27 | async-start | bytes 524288 | tf_op jit(solution)/shard_map/all_to_all | solution.py:43
  869.5 37.7 %copy-start.7 = (bf16[896,256]{0,1:T(8,128)(2,1)S(1)}, bf16[896,256]{0,1:T(8,128)(2,1)}, u32[]{:S(2)}) copy-start(bf16[896,256]{0,1:T(8,128)(2,1)} %copy-done.6) | copy-start | bytes 1376260
  881.5 18.0 %all-to-all-start.25 = ((f32[64,4,256]{2,1,0:T(4,128)}), f32[64,4,256]{2,1,0:T(4,128)S(1)}, u32[]{:S(2)}, u32[]{:S(2)}) async-start(f32[64,4,256]{2,1,0:T(4,128)} %reshape.87), calls=%async_computation.25 | async-start | bytes 524288 | tf_op jit(solution)/shard_map/all_to_all | solution.py:43
  900.2 18.0 %all-to-all-start.28 = ((f32[64,4,256]{2,1,0:T(4,128)}), f32[64,4,256]{2,1,0:T(4,128)S(1)}, u32[]{:S(2)}, u32[]{:S(2)}) async-start(f32[64,4,256]{2,1,0:T(4,128)} %broadcast_in_dim.64), calls=%async_computation.28 | async-start | bytes 524288 | tf_op jit(solution)/shard_map/all_to_all | solution.py:21
  919.0 67.3 %all-to-all-start.26 = ((f32[64,4,256]{2,1,0:T(4,128)}), f32[64,4,256]{2,1,0:T(4,128)S(1)}, u32[]{:S(2)}, u32[]{:S(2)}) async-start(f32[64,4,256]{2,1,0:T(4,128)} %broadcast_in_dim.63), calls=%async_computation.26 | async-start | bytes 524288 | tf_op jit(solution)/shard_map/all_to_all | solution.py:21
  986.3 3.9 copy-start.1
where the time goes:
time: 1000 us; the launch traced here: 990 us
  other arithmetic  291 us (29%)
  blocking collectives  194 us (19%)
  waiting for transfers between devices  182 us (18%)
  starting transfers between devices  171 us (17%)
  local copies, waits for them, and re-layouts  89.9 us (9%)
  matrix products  52.5 us (5%)
    psum x5, blocking collectives, project(): z_rows = lax.psum(partial_value, 'feat').astype(jnp.bfloat16)  147 us
    another operation x27, other arithmetic, half_step(): lower = jnp.linalg.cholesky(sums[0] / tokens)  139 us
    another operation x9, other arithmetic, half_step(): lax.linalg.triangular_solve(lower, cross, left_side=False, lower=True, tr...  82.8 us
    all_to_all x11, starting transfers between devices, copy_for_each(): return lax.all_to_all(copies, axis, split_axis=0, concat_axis=0, tiled=True)  77.8 us
    all_to_all x7, starting transfers between devices, summed_on_arrival(): lax.all_to_all(blocks, axis, split_axis=0, concat_axis=0, tiled=True)  73.2 us
    all_to_all x11, waiting for transfers between devices, copy_for_each(): return lax.all_to_all(copies, axis, split_axis=0, concat_axis=0, tiled=True)  70.8 us
    all_to_all x7, waiting for transfers between devices, summed_on_arrival(): lax.all_to_all(blocks, axis, split_axis=0, concat_axis=0, tiled=True)  58 us
    all_to_all x4, waiting for transfers between devices, sum_in_two_steps(): lax.all_to_all(nearer, far, split_axis=0, concat_axis=0, tiled=True)  53.4 us
  transfers between devices with their start and end apart: 22, of which 17 were waited for; matrix products, arithmetic and copies ran while one was open for 35% of the time, Pallas kernels for 0%

commit v1 on v0

v1 whole, which is shorter than its diff:
```python
import functools
import types

import jax
import jax.numpy as jnp
from jax import lax
from jax.experimental import pallas as pl
from jax.experimental.pallas import tpu as pltpu
from jax.sharding import Mesh
from jax.sharding import PartitionSpec as P

ITERS = 2
TOK = ("tok_0", "tok_1", "tok_2")
MESH = pl.DeviceIdType.MESH
HI = lax.Precision.HIGHEST
F32, BF16 = jnp.float32, jnp.bfloat16
PIECE = 16


def lane_of(tile, lane):
    return jnp.broadcast_to(tile[:, lane : lane + 1], (8, 128))


def row_of(tile, row):
    return jnp.broadcast_to(tile[row : row + 1, :], (8, 128))


def inverse_factor(block):
    sub = lax.broadcasted_iota(jnp.int32, (8, 128), 0)
    lane = lax.broadcasted_iota(jnp.int32, (8, 128), 1)
    n = 16
    left = [block[8 * i : 8 * i + 8, :] for i in range(n)]
    right = [jnp.where(lane == sub + 8 * i, 1.0, 0.0).astype(F32) for i in range(n)]
    for jb in range(n):
        col = {i: [lane_of(left[i], 8 * jb + k) for k in range(8)] for i in range(jb, n)}
        for k in range(8):
            head = col[jb][k]
            r = lax.rsqrt(row_of(head, k))
            rr = r * r
            row_l, row_r = row_of(left[jb], k), row_of(right[jb], k)
            for later in range(k + 1, 8):
                s = row_of(head, later)
                for i in range(jb, n):
                    col[i][later] = col[i][later] - (col[i][k] * s) * rr
            sl, sr = row_l * rr, row_r * rr
            low = jnp.where(sub > k, head, 0.0)
            left[jb] = jnp.where(sub == k, row_l * r, left[jb] - low * sl)
            right[jb] = jnp.where(sub == k, row_r * r, right[jb] - low * sr)
            for i in range(jb + 1, n):
                left[i] = left[i] - col[i][k] * sl
                right[i] = right[i] - col[i][k] * sr
    return jnp.concatenate(right, axis=0)


def mm(a, b, ca=1, cb=0, precision=HI):
    return lax.dot_general(
        a, b, (((ca,), (cb,)), ((), ())), precision=precision, preferred_element_type=F32
    )


def factor_into(g, blocks, low, inv):
    blocks[0] = g[0:128, 0:128]
    blocks[1] = g[128:256, 128:256]
    inv[0:128, 128:256] = jnp.zeros((128, 128), F32)

    def part(s, carry):
        blocks[s] = inverse_factor(blocks[s])

        @pl.when(s == 0)
        def _():
            p = mm(g[128:256, 0:128], blocks[0], 1, 1)
            low[...] = p
            blocks[1] = blocks[1] - mm(p, p, 1, 1)

        return carry

    lax.fori_loop(0, 2, part, 0)
    inv[0:128, 0:128] = blocks[0]
    inv[128:256, 128:256] = blocks[1]
    inv[128:256, 0:128] = -mm(blocks[1], mm(low[...], blocks[0]))


def solve_kernel(tokens, root, lane, g_ref, piece_ref, ss_ref, dirs_ref, inv_ref, blocks, low):
    factor_into(g_ref[...] * (1.0 / tokens), blocks, low, inv_ref)
    solved = mm(piece_ref[...] * (1.0 / tokens), inv_ref[...], 1, 1)
    scale = root / (ss_ref[:, lane : lane + 1] * (1.0 / tokens) + 0.5)
    dirs_ref[...] = (solved * scale).astype(BF16)


def final_kernel(tokens, g_ref, first_inv_ref, corr_ref, blocks, low, inv):
    factor_into(g_ref[0] * (1.0 / tokens), blocks, low, inv)
    left = mm(first_inv_ref[...], g_ref[1] * (1.0 / tokens))
    corr_ref[...] = mm(left, inv[...], 1, 1)


def in_vmem(n):
    return [pl.BlockSpec(memory_space=pltpu.VMEM)] * n


def factor_scratch():
    return [pltpu.VMEM((2, 128, 128), F32), pltpu.VMEM((128, 128), F32)]


def solve(tokens, root, lane, gram, piece, ss):
    k = gram.shape[-1]
    return pl.pallas_call(
        functools.partial(solve_kernel, tokens, root, lane),
        out_shape=(
            jax.ShapeDtypeStruct(piece.shape, BF16),
            jax.ShapeDtypeStruct((k, k), F32),
        ),
        in_specs=in_vmem(3),
        out_specs=tuple(in_vmem(2)),
        scratch_shapes=factor_scratch(),
        name="solve",
    )(gram, piece, ss)


def finish(tokens, grams, first_inv):
    k = first_inv.shape[-1]
    return pl.pallas_call(
        functools.partial(final_kernel, tokens),
        out_shape=jax.ShapeDtypeStruct((k, k), F32),
        in_specs=in_vmem(2),
        out_specs=in_vmem(1)[0],
        scratch_shapes=[*factor_scratch(), pltpu.VMEM((k, k), F32)],
        name="finish",
    )(grams, first_inv)


class Copies:
    def __init__(self):
        self.sends = []

    def put(self, src, dst, send, recv, device, when=None):
        copy = pltpu.make_async_remote_copy(
            src_ref=src, dst_ref=dst, send_sem=send, recv_sem=recv,
            device_id=device, device_id_type=MESH,
        )
        self.act(copy.start, when)
        self.sends.append((copy, when))

    def arrived(self, dst, send, recv, device, when=None):
        copy = pltpu.make_async_remote_copy(
            src_ref=dst, dst_ref=dst, send_sem=send, recv_sem=recv,
            device_id=device, device_id_type=MESH,
        )
        self.act(copy.wait_recv, when)

    def act(self, what, when):
        if when is None:
            what()
        else:
            pl.when(when)(what)

    def drain(self):
        for copy, when in self.sends:
            self.act(copy.wait_send, when)


def step_kernel(mode, names, *refs):
    ref = types.SimpleNamespace(**dict(zip(names, refs)))
    nx, ny, nz, nc = (lax.axis_size(a) for a in ("feat", "tok_0", "tok_1", "tok_2"))
    x, y, z, c = (lax.axis_index(a) for a in ("feat", "tok_0", "tok_1", "tok_2"))
    owners = nz - 1
    tokens = ref.src.shape[0]
    feats = ref.src.shape[1]
    per_y = owners * PIECE
    per_c = ny * per_y
    half, quarter = tokens // 2, tokens // 4
    k = 256
    ng = ref.gs.shape[0]

    def at(value, size, unit):
        return pl.ds(pl.multiple_of(value, unit), size)

    loads = []
    src_load = pltpu.make_async_copy(ref.src, ref.s, ref.load_sem.at[0])
    src_load.start()
    other = ref.tgt if mode != "last" else ref.first_t
    other_load = pltpu.make_async_copy(other, ref.u, ref.load_sem.at[1])
    other_load.start()

    plane = []
    for dx in range(nx):
        for dy in range(ny):
            for dc in range(nc):
                if dx or dy or dc:
                    plane.append((dx, dy, dc))

    def plane_peer(dx, dy, dc):
        return lax.rem(x + dx, nx), lax.rem(y + dy, ny), lax.rem(c + dc, nc)

    barrier = pltpu.get_barrier_semaphore()
    for d in plane:
        px, py, pc = plane_peer(*d)
        pl.semaphore_signal(
            barrier, inc=1, device_id={"feat": px, "tok_0": py, "tok_2": pc}, device_id_type=MESH
        )
    for d in range(1, nz):
        pl.semaphore_signal(
            barrier, inc=1, device_id={"tok_1": lax.rem(z + d, nz)}, device_id_type=MESH
        )
    pl.semaphore_wait(barrier, len(plane) + nz - 1)

    copies = Copies()

    if mode == "first":
        w = ref.dirs
    else:
        w = ref.w
        piece = ref.piece
        row = c * per_c + y * per_y
        owner = z < owners

        @pl.when(owner)
        def _():
            w[at(row + z * PIECE, PIECE, PIECE), :] = piece[...]

        for d in range(1, nz):
            copies.put(
                piece, w.at[at(row + lax.rem(z, owners) * PIECE, PIECE, PIECE)],
                ref.wz_s.at[d - 1], ref.wz_r.at[d - 1],
                {"tok_1": lax.rem(z + d, nz)}, owner,
            )
        for d in range(1, nz):
            sender = lax.rem(z + nz - d, nz)
            copies.arrived(
                w.at[at(row + lax.rem(sender, owners) * PIECE, PIECE, PIECE)],
                ref.wz_s.at[d - 1], ref.wz_r.at[d - 1], {"tok_1": sender}, sender < owners,
            )
        for d in range(1, ny):
            copies.put(
                w.at[at(row, per_y, PIECE)], w.at[at(row, per_y, PIECE)],
                ref.wy_s.at[d - 1], ref.wy_r.at[d - 1], {"tok_0": lax.rem(y + d, ny)},
            )
        for d in range(1, ny):
            sender = lax.rem(y + ny - d, ny)
            copies.arrived(
                w.at[at(c * per_c + sender * per_y, per_y, PIECE)],
                ref.wy_s.at[d - 1], ref.wy_r.at[d - 1], {"tok_0": sender},
            )
        for d in range(1, nc):
            copies.put(
                w.at[at(c * per_c, per_c, PIECE)], w.at[at(c * per_c, per_c, PIECE)],
                ref.wc_s.at[d - 1], ref.wc_r.at[d - 1], {"tok_2": lax.rem(c + d, nc)},
            )
        for d in range(1, nc):
            sender = lax.rem(c + nc - d, nc)
            copies.arrived(
                w.at[at(sender * per_c, per_c, PIECE)],
                ref.wc_s.at[d - 1], ref.wc_r.at[d - 1], {"tok_2": sender},
            )

    src_load.wait()
    part, out = ref.part, ref.out

    def project(i, carry):
        rows = at(i * quarter, quarter, 16)
        value = jnp.dot(ref.s[rows, :], w[...], preferred_element_type=F32)
        part[rows, :] = value
        out[0, rows, :] = value[:, 0:128].astype(BF16)
        out[1, rows, :] = value[:, 128:256].astype(BF16)
        return carry

    lax.fori_loop(0, 4, project, 0)

    near = x + 1 - 2 * lax.rem(x, 2)
    far = nx - 1 - x
    high, odd = x // 2, lax.rem(x, 2)
    plans = (
        (lax.rem(high + odd, 2), high, near, far),
        (high, odd, far, near),
    )
    zf = ref.z
    for i, (k1, k2, one, two) in enumerate(plans):
        copies.put(
            out.at[i, at((1 - k1) * half, half, 16)], ref.r1.at[i],
            ref.x_s.at[i, 0], ref.x_r.at[i, 0], {"feat": one},
        )
    other_load.wait()
    if mode == "first":
        for j in range(feats // 128):
            cols = slice(j * 128, j * 128 + 128)
            def square_sum(value):
                return jnp.sum(jnp.square(value.astype(F32)), axis=0, keepdims=True)
            first = square_sum(ref.u[:, cols])
            second = square_sum(ref.s[:, cols])
            upper = lax.broadcasted_iota(jnp.int32, (128, 128), 0) < 64
            both = jnp.where(upper, jnp.broadcast_to(first, (128, 128)), jnp.broadcast_to(second, (128, 128)))
            ref.sb[cols, :] = both.T
    for i, (k1, k2, one, two) in enumerate(plans):
        copies.arrived(ref.r1.at[i], ref.x_s.at[i, 0], ref.x_r.at[i, 0], {"feat": one})
        lanes = slice(i * 128, i * 128 + 128)
        give = (1 - k2) * quarter
        value = part[at(k1 * half + give, quarter, 16), lanes] + ref.r1[i, at(give, quarter, 16), :].astype(F32)
        ref.g2[i] = value.astype(BF16)
        copies.put(
            ref.g2.at[i], ref.r2.at[i], ref.x_s.at[i, 1], ref.x_r.at[i, 1], {"feat": two}
        )
    for i, (k1, k2, one, two) in enumerate(plans):
        lanes = slice(i * 128, i * 128 + 128)
        keep = k2 * quarter
        value = part[at(k1 * half + keep, quarter, 16), lanes] + ref.r1[i, at(keep, quarter, 16), :].astype(F32)
        copies.arrived(ref.r2.at[i], ref.x_s.at[i, 1], ref.x_r.at[i, 1], {"feat": two})
        mine = at(k1 * half + keep, quarter, 16)
        zf[i, mine, :] = (value + ref.r2[i].astype(F32)).astype(BF16)
        copies.put(
            zf.at[i, mine], zf.at[i, mine], ref.x_s.at[i, 2], ref.x_r.at[i, 2], {"feat": two}
        )
    for i, (k1, k2, one, two) in enumerate(plans):
        copies.arrived(
            zf.at[i, at(k1 * half + (1 - k2) * quarter, quarter, 16)],
            ref.x_s.at[i, 2], ref.x_r.at[i, 2], {"feat": two},
        )
        mine = at(k1 * half, half, 16)
        copies.put(
            zf.at[i, mine], zf.at[i, mine], ref.x_s.at[i, 3], ref.x_r.at[i, 3], {"feat": one}
        )
    for i, (k1, k2, one, two) in enumerate(plans):
        copies.arrived(
            zf.at[i, at((1 - k1) * half, half, 16)],
            ref.x_s.at[i, 3], ref.x_r.at[i, 3], {"feat": one},
        )

    zt = ref.zt
    for i in range(2):
        zt[i * 128 : i * 128 + 128, :] = zf[i].T
    gs = ref.gs
    rows = at(x * 64, 64, 16)
    lefts = [zt[rows, :]] + ([ref.u[rows, :]] if mode == "last" else [])
    for n, left in enumerate(lefts):
        for i in range(2):
            gs[n, :, i * 128 : i * 128 + 128] = jnp.dot(left, zf[i], preferred_element_type=F32)
    for d in range(1, nc):
        peer = lax.rem(c + d, nc)
        copies.put(
            gs.at[:, at(peer * 32, 32, 8)], ref.rgc.at[d - 1],
            ref.gc_s.at[d - 1], ref.gc_r.at[d - 1], {"tok_2": peer},
        )
    crossed = mode != "last"
    if crossed:
        cb = ref.cb
        for lo in range(0, feats, 256):
            hi = min(lo + 256, feats)
            value = jnp.dot(zt[...], ref.u[:, lo:hi], preferred_element_type=F32)
            cb[lo:hi, :] = value.T
        for d in range(1, nc):
            peer = lax.rem(c + d, nc)
            copies.put(
                cb.at[at(peer * per_c, per_c, PIECE)], ref.rcc.at[d - 1],
                ref.cc_s.at[d - 1], ref.cc_r.at[d - 1], {"tok_2": peer},
            )
            if mode == "first":
                copies.put(
                    ref.sb.at[at(peer * per_c, per_c, PIECE)], ref.rsc.at[d - 1],
                    ref.sc_s.at[d - 1], ref.sc_r.at[d - 1], {"tok_2": peer},
                )

    gram = gs[:, at(c * 32, 32, 8), :]
    for d in range(1, nc):
        sender = {"tok_2": lax.rem(c + nc - d, nc)}
        copies.arrived(ref.rgc.at[d - 1], ref.gc_s.at[d - 1], ref.gc_r.at[d - 1], sender)
        gram = gram + ref.rgc[d - 1]
    ref.gy[...] = gram
    for d in range(1, ny):
        peer = lax.rem(y + d, ny)
        copies.put(
            ref.gy.at[:, at(peer * 8, 8, 8)], ref.rgy.at[d - 1],
            ref.gy_s.at[d - 1], ref.gy_r.at[d - 1], {"tok_0": peer},
        )
    if crossed:
        own = at(c * per_c, per_c, PIECE)
        cross = cb[own, :]
        for d in range(1, nc):
            sender = {"tok_2": lax.rem(c + nc - d, nc)}
            copies.arrived(ref.rcc.at[d - 1], ref.cc_s.at[d - 1], ref.cc_r.at[d - 1], sender)
            cross = cross + ref.rcc[d - 1]
        ref.cy[...] = cross
        if mode == "first":
            sums = ref.sb[own, :]
            for d in range(1, nc):
                sender = {"tok_2": lax.rem(c + nc - d, nc)}
                copies.arrived(ref.rsc.at[d - 1], ref.sc_s.at[d - 1], ref.sc_r.at[d - 1], sender)
                sums = sums + ref.rsc[d - 1]
            ref.sy[...] = sums
        for d in range(1, ny):
            peer = lax.rem(y + d, ny)
            copies.put(
                ref.cy.at[at(peer * per_y, per_y, PIECE)], ref.rcy.at[d - 1],
                ref.cy_s.at[d - 1], ref.cy_r.at[d - 1], {"tok_0": peer},
            )
            if mode == "first":
                copies.put(
                    ref.sy.at[at(peer * per_y, per_y, PIECE)], ref.rsy.at[d - 1],
                    ref.sy_s.at[d - 1], ref.sy_r.at[d - 1], {"tok_0": peer},
                )
    gram = ref.gy[:, at(y * 8, 8, 8), :]
    for d in range(1, ny):
        sender = {"tok_0": lax.rem(y + ny - d, ny)}
        copies.arrived(ref.rgy.at[d - 1], ref.gy_s.at[d - 1], ref.gy_r.at[d - 1], sender)
        gram = gram + ref.rgy[d - 1]
    ref.gz[...] = gram
    for d in range(1, nz):
        copies.put(
            ref.gz, ref.rgz.at[d - 1], ref.gz_s.at[d - 1], ref.gz_r.at[d - 1],
            {"tok_1": lax.rem(z + d, nz)},
        )
    if crossed:
        own = at(y * per_y, per_y, PIECE)
        cross = ref.cy[own, :]
        for d in range(1, ny):
            sender = {"tok_0": lax.rem(y + ny - d, ny)}
            copies.arrived(ref.rcy.at[d - 1], ref.cy_s.at[d - 1], ref.cy_r.at[d - 1], sender)
            cross = cross + ref.rcy[d - 1]
        ref.cz[...] = cross
        if mode == "first":
            sums = ref.sy[own, :]
            for d in range(1, ny):
                sender = {"tok_0": lax.rem(y + ny - d, ny)}
                copies.arrived(ref.rsy.at[d - 1], ref.sy_s.at[d - 1], ref.sy_r.at[d - 1], sender)
                sums = sums + ref.rsy[d - 1]
            ref.sz[...] = sums
        for d in range(1, nz):
            peer = lax.rem(z + d, nz)
            rows = at(lax.rem(peer, owners) * PIECE, PIECE, PIECE)
            copies.put(
                ref.cz.at[rows], ref.rcz.at[d - 1],
                ref.cz_s.at[d - 1], ref.cz_r.at[d - 1], {"tok_1": peer}, peer < owners,
            )
            if mode == "first":
                copies.put(
                    ref.sz.at[rows], ref.rsz.at[d - 1],
                    ref.sz_s.at[d - 1], ref.sz_r.at[d - 1], {"tok_1": peer}, peer < owners,
                )

    gram = ref.gz[...]
    for d in range(1, nz):
        sender = {"tok_1": lax.rem(z + nz - d, nz)}
        copies.arrived(ref.rgz.at[d - 1], ref.gz_s.at[d - 1], ref.gz_r.at[d - 1], sender)
        gram = gram + ref.rgz[d - 1]

    def place(px, py, pc):
        return (px * nc + pc) * ny + py

    ga = ref.ga
    mine = place(x, y, c)
    ref.gm[...] = gram
    ga[mine] = gram
    for i, d in enumerate(plane):
        px, py, pc = plane_peer(*d)
        copies.put(
            ref.gm, ga.at[mine], ref.ga_s.at[i], ref.ga_r.at[i],
            {"feat": px, "tok_0": py, "tok_2": pc},
        )
    if crossed:
        @pl.when(z < owners)
        def _():
            rows = at(lax.rem(z, owners) * PIECE, PIECE, PIECE)
            cross = ref.cz[rows, :]
            for d in range(1, nz):
                sender = {"tok_1": lax.rem(z + nz - d, nz)}
                copies.arrived(ref.rcz.at[d - 1], ref.cz_s.at[d - 1], ref.cz_r.at[d - 1], sender)
                cross = cross + ref.rcz[d - 1]
            ref.cross[...] = cross
            if mode == "first":
                sums = ref.sz[rows, :]
                for d in range(1, nz):
                    sender = {"tok_1": lax.rem(z + nz - d, nz)}
                    copies.arrived(ref.rsz.at[d - 1], ref.sz_s.at[d - 1], ref.sz_r.at[d - 1], sender)
                    sums = sums + ref.rsz[d - 1]
                ref.ss[...] = sums

        @pl.when(z >= owners)
        def _():
            ref.cross[...] = jnp.zeros_like(ref.cross)
            if mode == "first":
                ref.ss[...] = jnp.zeros_like(ref.ss)

    if mode == "mid":
        ref.z_t[...] = zt[...]
    if mode != "first":
        ref.w_out[...] = w[...]
    for i, (dx, dy, dc) in enumerate(plane):
        px, py, pc = lax.rem(x + nx - dx, nx), lax.rem(y + ny - dy, ny), lax.rem(c + nc - dc, nc)
        copies.arrived(
            ga.at[place(px, py, pc)], ref.ga_s.at[i], ref.ga_r.at[i],
            {"feat": px, "tok_0": py, "tok_2": pc},
        )
    for g in range(nx * ny * nc):
        for n in range(ng):
            ref.gram[n, g * 8 : g * 8 + 8, :] = ga[g, n]
    copies.drain()


def step(mode, collective_id, source, target, dirs, sizes):
    nx, ny, nz, nc = sizes
    tokens, feats = source.shape
    k = 256
    owners = nz - 1
    per_y = owners * PIECE
    per_c = ny * per_y
    assert per_c * nc == feats and nx == 4
    ng = 2 if mode == "last" else 1
    half, quarter = tokens // 2, tokens // 4
    vmem, hbm = pl.BlockSpec(memory_space=pltpu.VMEM), pl.BlockSpec(memory_space=pl.ANY)
    dma = pltpu.SemaphoreType.DMA

    ins = [("src", hbm), ("first_t" if mode == "last" else "tgt", hbm)]
    ins.append(("dirs" if mode == "first" else "piece", vmem))
    outs = [("gram", (ng, k, k), F32)]
    if mode != "first":
        outs.append(("w_out", (feats, k), BF16))
    if mode != "last":
        outs.append(("cross", (PIECE, k), F32))
    if mode == "first":
        outs.append(("ss", (PIECE, 128), F32))
    if mode == "mid":
        outs.append(("z_t", (k, tokens), BF16))
    scratch = dict(
        s=pltpu.VMEM((tokens, feats), BF16),
        u=pltpu.VMEM(target.shape, BF16),
        load_sem=dma((2,)),
        part=pltpu.VMEM((tokens, k), F32),
        out=pltpu.VMEM((2, tokens, 128), BF16),
        z=pltpu.VMEM((2, tokens, 128), BF16),
        zt=pltpu.VMEM((k, tokens), BF16),
        r1=pltpu.VMEM((2, half, 128), BF16),
        g2=pltpu.VMEM((2, quarter, 128), BF16),
        r2=pltpu.VMEM((2, quarter, 128), BF16),
        x_s=dma((2, 4)),
        x_r=dma((2, 4)),
        gs=pltpu.VMEM((ng, 64, k), F32),
        rgc=pltpu.VMEM((nc - 1, ng, 32, k), F32),
        gy=pltpu.VMEM((ng, 32, k), F32),
        rgy=pltpu.VMEM((ny - 1, ng, 8, k), F32),
        gz=pltpu.VMEM((ng, 8, k), F32),
        rgz=pltpu.VMEM((nz - 1, ng, 8, k), F32),
        gm=pltpu.VMEM((ng, 8, k), F32),
        ga=pltpu.VMEM((nx * ny * nc, ng, 8, k), F32),
        gc_s=dma((nc - 1,)), gc_r=dma((nc - 1,)),
        gy_s=dma((ny - 1,)), gy_r=dma((ny - 1,)),
        gz_s=dma((nz - 1,)), gz_r=dma((nz - 1,)),
        ga_s=dma((nx * ny * nc - 1,)), ga_r=dma((nx * ny * nc - 1,)),
    )
    if mode != "first":
        scratch |= dict(
            w=pltpu.VMEM((feats, k), BF16),
            wz_s=dma((nz - 1,)), wz_r=dma((nz - 1,)),
            wy_s=dma((ny - 1,)), wy_r=dma((ny - 1,)),
            wc_s=dma((nc - 1,)), wc_r=dma((nc - 1,)),
        )
    kinds = []
    if mode != "last":
        kinds.append(("c", k, F32))
        scratch["cb"] = pltpu.VMEM((feats, k), F32)
    if mode == "first":
        kinds.append(("s", 128, F32))
        scratch["sb"] = pltpu.VMEM((feats, 128), F32)
    for name, lanes, kind in kinds:
        scratch |= {
            "r" + name + "c": pltpu.VMEM((nc - 1, per_c, lanes), kind),
            name + "y": pltpu.VMEM((per_c, lanes), kind),
            "r" + name + "y": pltpu.VMEM((ny - 1, per_y, lanes), kind),
            name + "z": pltpu.VMEM((per_y, lanes), F32),
            "r" + name + "z": pltpu.VMEM((nz - 1, PIECE, lanes), F32),
            name + "c_s": dma((nc - 1,)), name + "c_r": dma((nc - 1,)),
            name + "y_s": dma((ny - 1,)), name + "y_r": dma((ny - 1,)),
            name + "z_s": dma((nz - 1,)), name + "z_r": dma((nz - 1,)),
        }
    names = [n for n, _ in ins] + [n for n, _, _ in outs] + list(scratch)
    values = pl.pallas_call(
        functools.partial(step_kernel, mode, names),
        out_shape=tuple(jax.ShapeDtypeStruct(s, d) for _, s, d in outs),
        in_specs=[spec for _, spec in ins],
        out_specs=tuple(vmem for _ in outs),
        scratch_shapes=list(scratch.values()),
        compiler_params=pltpu.CompilerParams(collective_id=collective_id, has_side_effects=True),
        name="step_" + mode,
    )(source, target, dirs)
    return dict(zip([n for n, _, _ in outs], values))


def body(first_acts, second_acts, start_dirs):
    sizes = tuple(lax.axis_size(a) for a in ("feat", *TOK))
    tokens = float(first_acts.shape[0] * lax.axis_size(TOK))
    root = float(first_acts.shape[1] * sizes[0]) ** 0.5
    acts = (first_acts, second_acts)
    got = step("first", 0, second_acts, first_acts, start_dirs, sizes)
    ss = got["ss"]
    dirs = [None, None]
    for h in range(2 * ITERS):
        side = h % 2
        piece, inverse = solve(tokens, root, 64 * side, got["gram"][0], got["cross"], ss)
        if h < 2 * ITERS - 1:
            got = step("mid", 1, acts[side], acts[1 - side], piece, sizes)
        else:
            got = step("last", 2, second_acts, got["z_t"], piece, sizes)
        dirs[side] = got["w_out"]
    return (dirs[0], dirs[1], finish(tokens, got["gram"], inverse))


def solution(mesh):
    split = Mesh(
        mesh.devices.reshape(4, 8, 2, mesh.shape["feat"]), ("tok_0", "tok_1", "tok_2", "feat")
    )
    in_specs = (P(TOK, "feat"), P(TOK, "feat"), P("feat", None))
    out_specs = (P("feat", None), P("feat", None), P())
    return jax.shard_map(body, mesh=split, in_specs=in_specs, out_specs=out_specs, check_vma=False)
```

time: 1000 us -> 329 us (0.33)
  Pallas kernels: 0 us -> 326 us
  other arithmetic: 291 us -> 0 us
  blocking collectives: 194 us -> 0 us
  waiting for transfers between devices: 182 us -> 0 us
  starting transfers between devices: 171 us -> 0 us
  local copies, waits for them, and re-layouts: 89.9 us -> 2.59 us
  matrix products: 52.5 us -> 0 us
    pallas_call x0 -> x10, Pallas kernels: none -> 326 us  [the longest x5 270 us: step(): pl.pallas_call(functools.partial(step_kernel, mode, names), out_shape=tup...]
    another operation x46 -> x0, other arithmetic: 276 us -> none  [the longest x27 139 us: half_step(): lower = jnp.linalg.cholesky(sums[0] / tokens)]
    all_to_all x22 -> x0, waiting for transfers between devices: 182 us -> none  [the longest x11 70.8 us: copy_for_each(): return lax.all_to_all(copies, axis, split_axis=0, concat_axis=0, tiled=True)]
    all_to_all x22 -> x0, starting transfers between devices: 171 us -> none  [the longest x11 77.8 us: copy_for_each(): return lax.all_to_all(copies, axis, split_axis=0, concat_axis=0, tiled=True)]
    psum x5 -> x0, blocking collectives: 147 us -> none  [project(): z_rows = lax.psum(partial_value, 'feat').astype(jnp.bfloat16)]
    all_to_all x7 -> x0, blocking collectives: 47.1 us -> none  [the longest x3 27.4 us: summed_on_arrival(): lax.all_to_all(blocks, axis, split_axis=0, concat_axis=0, tiled=True)]
    another operation x28 -> x0, matrix products: 29.6 us -> none  [the longest x12 17.1 us: half_step(): lax.linalg.triangular_solve(lower, cross, left_side=False, lower=True, tr...]
    another operation x53 -> x0, local copies, waits for them, and re-layouts: 27.6 us -> none  [the longest x30 17.7 us: half_step(): lax.linalg.triangular_solve(lower, cross, left_side=False, lower=True, tr...]
  transfers between devices with their start and end apart: 22 -> 0, of which waited for: 17 -> 0; matrix products, arithmetic and copies ran while one was open for 35% -> 0% of each run, Pallas kernels for 0% -> 0%
where the time goes in v1:
time: 329 us
  Pallas kernels  326 us (99%)
    pallas_call x5, Pallas kernels, step(): pl.pallas_call(functools.partial(step_kernel, mode, names), out_shape=tup...  270 us
    pallas_call x4, Pallas kernels, solve(): pl.pallas_call(functools.partial(solve_kernel, tokens, root, lane), out_s...  43.9 us
    pallas_call x1, Pallas kernels, finish(): pl.pallas_call(functools.partial(final_kernel, tokens), out_shape=jax.Sha...  11.8 us

profile of v1, /device:TPU:1, one launch (start us, length us, event | category | flops | bytes accessed | tf_op | source)
XLA Modules:
  0.0 329.0 jit_solution(11616622094711160244)
XLA Ops:
  0.6 51.6 %step_first.1 = (f32[1,256,256]{2,1,0:T(8,128)}, f32[16,256]{1,0:T(8,128)}, f32[16,128]{1,0:T(8,128)}) custom-call(bf16[1280,896]{1,0:T(8,128)(2,1)} %refs_0_.9, bf16[1280,896]{1,0:T(8,128)(2,1)} %refs_0_.8, bf16[896,256]{1,0:T(8,128)(2,1)} %refs_2_.1), custom_call_target="tpu_custom_call" | custom-call | tf_op jit(solution)/shard_map/step_first/pallas_call | solution.py:572
  52.2 11.0 %solve.4 = (bf16[16,256]{1,0:T(8,128)(2,1)}, f32[256,256]{1,0:T(8,128)}) custom-call(f32[256,256]{1,0:T(8,128)} %bitcast.7, f32[16,256]{1,0:T(8,128)} %get-tuple-element.22.piece_ref, f32[16,128]{1,0:T(8,128)} %get-tuple-element.23.ss_ref), custom_call_target="tpu_custom_call" | custom-call | tf_op jit(solution)/shard_map/solve/pallas_call | solution.py:106
  63.2 54.2 %step_mid.3 = (f32[1,256,256]{2,1,0:T(8,128)}, bf16[896,256]{1,0:T(8,128)(2,1)}, f32[16,256]{1,0:T(8,128)}, bf16[256,1280]{1,0:T(8,128)(2,1)}) custom-call(bf16[1280,896]{1,0:T(8,128)(2,1)} %refs_0_.8, bf16[1280,896]{1,0:T(8,128)(2,1)} %refs_0_.9, bf16[16,256]{1,0:T(8,128)(2,1)} %get-tuple-element.24.refs_2_), custom_call_target="tpu_custom_call" | custom-call | tf_op jit(solution)/shard_map/step_mid/pallas_call | solution.py:572
  117.4 11.0 %solve.5 = (bf16[16,256]{1,0:T(8,128)(2,1)}, f32[256,256]{1,0:T(8,128)}) custom-call(f32[256,256]{1,0:T(8,128)} %bitcast.5, f32[16,256]{1,0:T(8,128)} %get-tuple-element.26.piece_ref, f32[16,128]{1,0:T(8,128)} %get-tuple-element.23.ss_ref), custom_call_target="tpu_custom_call" | custom-call | tf_op jit(solution)/shard_map/solve/pallas_call | solution.py:106
  128.4 53.5 %step_mid.4 = (f32[1,256,256]{2,1,0:T(8,128)}, bf16[896,256]{1,0:T(8,128)(2,1)}, f32[16,256]{1,0:T(8,128)}, bf16[256,1280]{1,0:T(8,128)(2,1)}) custom-call(bf16[1280,896]{1,0:T(8,128)(2,1)} %refs_0_.9, bf16[1280,896]{1,0:T(8,128)(2,1)} %refs_0_.8, bf16[16,256]{1,0:T(8,128)(2,1)} %get-tuple-element.27.refs_2_), custom_call_target="tpu_custom_call" | custom-call | tf_op jit(solution)/shard_map/step_mid/pallas_call | solution.py:572
  182.0 11.0 %solve.6 = (bf16[16,256]{1,0:T(8,128)(2,1)}, f32[256,256]{1,0:T(8,128)}) custom-call(f32[256,256]{1,0:T(8,128)} %bitcast.6, f32[16,256]{1,0:T(8,128)} %get-tuple-element.29.piece_ref, f32[16,128]{1,0:T(8,128)} %get-tuple-element.23.ss_ref), custom_call_target="tpu_custom_call" | custom-call | tf_op jit(solution)/shard_map/solve/pallas_call | solution.py:106
  192.9 53.8 %step_mid.5 = (f32[1,256,256]{2,1,0:T(8,128)}, bf16[896,256]{1,0:T(8,128)(2,1)}, f32[16,256]{1,0:T(8,128)}, bf16[256,1280]{1,0:T(8,128)(2,1)}) custom-call(bf16[1280,896]{1,0:T(8,128)(2,1)} %refs_0_.8, bf16[1280,896]{1,0:T(8,128)(2,1)} %refs_0_.9, bf16[16,256]{1,0:T(8,128)(2,1)} %get-tuple-element.30.refs_2_), custom_call_target="tpu_custom_call" | custom-call | tf_op jit(solution)/shard_map/step_mid/pallas_call | solution.py:572
  246.7 0.0 copy-start
  246.7 11.0 %solve.7 = (bf16[16,256]{1,0:T(8,128)(2,1)}, f32[256,256]{1,0:T(8,128)}) custom-call(f32[256,256]{1,0:T(8,128)} %bitcast.4, f32[16,256]{1,0:T(8,128)} %get-tuple-element.34.piece_ref, f32[16,128]{1,0:T(8,128)} %get-tuple-element.23.ss_ref), custom_call_target="tpu_custom_call" | custom-call | tf_op jit(solution)/shard_map/solve/pallas_call | solution.py:106
  257.7 56.9 %step_last.1 = (f32[2,256,256]{2,1,0:T(8,128)}, bf16[896,256]{1,0:T(8,128)(2,1)}) custom-call(bf16[1280,896]{1,0:T(8,128)(2,1)} %refs_0_.9, bf16[256,1280]{1,0:T(8,128)(2,1)} %get-tuple-element.32.refs_1_, bf16[16,256]{1,0:T(8,128)(2,1)} %get-tuple-element.35.refs_2_), custom_call_target="tpu_custom_call" | custom-call | tf_op jit(solution)/shard_map/step_last/pallas_call | solution.py:572
  314.6 11.8 %finish.1 = f32[256,256]{1,0:T(8,128)} custom-call(f32[2,256,256]{2,1,0:T(8,128)} %get-tuple-element.37.g_ref, f32[256,256]{1,0:T(8,128)} %get-tuple-element.38.first_inv_ref), custom_call_target="tpu_custom_call" | custom-call | tf_op jit(solution)/shard_map/finish/pallas_call | solution.py:121
  326.4 0.0 copy-done
  326.4 0.8 copy.8
  327.2 1.8 copy.9
Async XLA Ops:
  246.7 79.7 %copy-start = (bf16[896,256]{1,0:T(8,128)(2,1)S(1)}, bf16[896,256]{1,0:T(8,128)(2,1)}, u32[]{:S(2)}) copy-start(bf16[896,256]{1,0:T(8,128)(2,1)} %get-tuple-element.42) | copy-start | bytes 1376260

commit v2 on v0

v2 whole, which is shorter than its diff:
```python
import functools
import types

import jax
import jax.numpy as jnp
from jax import lax
from jax.experimental import pallas as pl
from jax.experimental.pallas import tpu as pltpu
from jax.sharding import Mesh
from jax.sharding import PartitionSpec as P

ITERS = 2
STEPS = 2 * ITERS
CHUNKS = 2
TOK = ("tok_0", "tok_1", "tok_2")
MESH = pl.DeviceIdType.MESH
HI = lax.Precision.HIGHEST
F32, BF16 = jnp.float32, jnp.bfloat16
PIECE = 16


def inverse_factor(block, between=None):
    n = block.shape[0]
    sub = lax.broadcasted_iota(jnp.int32, (8, n), 0)
    left = block
    right = jnp.where(
        lax.broadcasted_iota(jnp.int32, (n, n), 0) == lax.broadcasted_iota(jnp.int32, (n, n), 1), 1.0, 0.0
    ).astype(F32)
    done = []
    for j in range(0, n, 8):
        if between is not None and j == n // 2:
            between()
        head_l, head_r = left[0:8], right[0:8]
        rest_l, rest_r = left[8:], right[8:]
        more = j + 8 < n
        head = [jnp.broadcast_to(head_l[:, j + k : j + k + 1], (8, n)) for k in range(8)]
        if more:
            rest = [jnp.broadcast_to(rest_l[:, j + k : j + k + 1], rest_l.shape) for k in range(8)]
        for k in range(8):
            r = lax.rsqrt(head[k][k : k + 1, :])
            rr = r * r
            row_l, row_r = head_l[k : k + 1, :], head_r[k : k + 1, :]
            for later in range(k + 1, 8):
                s = head[k][later : later + 1, :]
                head[later] = head[later] - (head[k] * s) * rr
                if more:
                    rest[later] = rest[later] - (rest[k] * s) * rr
            sl, sr = row_l * rr, row_r * rr
            low = jnp.where(sub > k, head[k], 0.0)
            head_l = jnp.where(sub == k, row_l * r, head_l - low * sl)
            head_r = jnp.where(sub == k, row_r * r, head_r - low * sr)
            if more:
                rest_l = rest_l - rest[k] * sl
                rest_r = rest_r - rest[k] * sr
        done.append(head_r)
        left, right = rest_l, rest_r
    return jnp.concatenate(done, axis=0)


def mm(a, b, ca=1, cb=0, precision=HI):
    return lax.dot_general(
        a, b, (((ca,), (cb,)), ((), ())), precision=precision, preferred_element_type=F32
    )


def inverse_into(g, scale, inv, between=None):
    one = inverse_factor(g[0:128, 0:128] * scale)
    inv[0:128, 0:128] = one
    inv[0:128, 128:256] = jnp.zeros((128, 128), F32)
    p = mm(g[128:256, 0:128] * scale, one, 1, 1)
    inv[128:256, 0:128] = mm(p, one)
    two = inverse_factor(g[128:256, 128:256] * scale - mm(p, p, 1, 1), between)
    inv[128:256, 128:256] = two
    inv[128:256, 0:128] = -mm(two, inv[128:256, 0:128])


def split(value):
    high = value.astype(BF16)
    return high, (value - high.astype(F32)).astype(BF16)


class Copies:
    def __init__(self):
        self.sends = []

    def put(self, src, dst, send, recv, device, when=None):
        copy = pltpu.make_async_remote_copy(
            src_ref=src, dst_ref=dst, send_sem=send, recv_sem=recv,
            device_id=device, device_id_type=MESH,
        )
        self.act(copy.start, when)
        self.sends.append((copy, when))

    def arrived(self, dst, send, recv, device, when=None):
        copy = pltpu.make_async_remote_copy(
            src_ref=dst, dst_ref=dst, send_sem=send, recv_sem=recv,
            device_id=device, device_id_type=MESH,
        )
        self.act(copy.wait_recv, when)

    def act(self, what, when):
        if when is None:
            what()
        else:
            pl.when(when)(what)

    def drain(self):
        for copy, when in self.sends:
            self.act(copy.wait_send, when)


def kernel(names, total_tokens, root, *refs):
    ref = types.SimpleNamespace(**dict(zip(names, refs)))
    nx, ny, nz, nc = (lax.axis_size(a) for a in ("feat", *TOK))
    x, y, z, c = (lax.axis_index(a) for a in ("feat", *TOK))
    owners = nz - 1
    tokens, feats = ref.first_acts.shape
    per_y = owners * PIECE
    per_c = ny * per_y
    chunk = tokens // CHUNKS
    half, quarter = chunk // 2, chunk // 4
    count = 1.0 / total_tokens

    def at(value, size, unit):
        return pl.ds(pl.multiple_of(value, unit), size)

    loads = [
        pltpu.make_async_copy(ref.start_dirs, ref.w, ref.load_sem.at[0]),
        pltpu.make_async_copy(ref.second_acts, ref.acts.at[1], ref.load_sem.at[1]),
        pltpu.make_async_copy(ref.first_acts, ref.acts.at[0], ref.load_sem.at[2]),
    ]
    for load in loads:
        load.start()

    plane = [
        (dx, dy, dc)
        for dx in range(nx) for dy in range(ny) for dc in range(nc) if dx or dy or dc
    ]

    def on_plane(dx, dy, dc):
        px, py, pc = lax.rem(x + dx + nx, nx), lax.rem(y + dy + ny, ny), lax.rem(c + dc + nc, nc)
        return (px, py, pc), {"feat": px, "tok_0": py, "tok_2": pc}

    def place(px, py, pc):
        return (px * nc + pc) * ny + py

    def after(i, d, n):
        return lax.rem(i + d, n)

    def before(i, d, n):
        return lax.rem(i + n - d, n)

    barrier = pltpu.get_barrier_semaphore()
    for d in plane:
        pl.semaphore_signal(barrier, inc=1, device_id=on_plane(*d)[1], device_id_type=MESH)
    for d in range(1, nz):
        pl.semaphore_signal(barrier, inc=1, device_id={"tok_1": after(z, d, nz)}, device_id_type=MESH)
    pl.semaphore_wait(barrier, len(plane) + nz - 1)

    near = x + 1 - 2 * lax.rem(x, 2)
    far = nx - 1 - x
    high, odd = x // 2, lax.rem(x, 2)
    ways = ((lax.rem(high + odd, 2), high, near, far), (high, odd, far, near))
    plans = [(u * 2 + i, u * chunk, i, *ways[i]) for u in range(CHUNKS) for i in range(2)]

    def column_sums():
        for j in range(feats // 128):
            cols = slice(j * 128, j * 128 + 128)
            first, second = (
                jnp.sum(jnp.square(ref.acts[i, :, cols].astype(F32)), axis=0, keepdims=True)
                for i in range(2)
            )
            upper = lax.broadcasted_iota(jnp.int32, (128, 128), 0) < 64
            ref.sb[cols, :] = jnp.where(
                upper, jnp.broadcast_to(first, (128, 128)), jnp.broadcast_to(second, (128, 128))
            ).T

    def projected(h, source, zf, copies, first_time, beside):
        for u in range(CHUNKS):

            def project(i, carry):
                rows = at(u * chunk + i * half, half, 16)
                value = jnp.dot(source[rows, :], ref.w[...], preferred_element_type=F32)
                ref.part[rows, :] = value
                ref.out[0, rows, :] = value[:, 0:128].astype(BF16)
                ref.out[1, rows, :] = value[:, 128:256].astype(BF16)
                return carry

            lax.fori_loop(0, 2, project, 0)
            for p, base, i, k1, k2, one, two in plans[2 * u : 2 * u + 2]:
                copies.put(
                    ref.out.at[i, at(base + (1 - k1) * half, half, 16)], ref.r1.at[h, p],
                    ref.x_s.at[p, 0], ref.x_r.at[h, p, 0], {"feat": one},
                )
        beside()
        for p, base, i, k1, k2, one, two in plans:
            copies.arrived(ref.r1.at[h, p], ref.x_s.at[p, 0], ref.x_r.at[h, p, 0], {"feat": one})
            lanes = slice(i * 128, i * 128 + 128)
            give = (1 - k2) * quarter
            value = ref.part[at(base + k1 * half + give, quarter, 16), lanes]
            ref.g2[p] = (value + ref.r1[h, p, at(give, quarter, 16), :].astype(F32)).astype(BF16)
            copies.put(
                ref.g2.at[p], ref.r2.at[h, p], ref.x_s.at[p, 1], ref.x_r.at[h, p, 1], {"feat": two}
            )
        for p, base, i, k1, k2, one, two in plans:
            lanes = slice(i * 128, i * 128 + 128)
            keep = k2 * quarter
            mine = at(base + k1 * half + keep, quarter, 16)
            value = ref.part[mine, lanes] + ref.r1[h, p, at(keep, quarter, 16), :].astype(F32)
            copies.arrived(ref.r2.at[h, p], ref.x_s.at[p, 1], ref.x_r.at[h, p, 1], {"feat": two})
            zf[i, mine, :] = (value + ref.r2[h, p].astype(F32)).astype(BF16)
            copies.put(
                zf.at[i, mine], zf.at[i, mine], ref.x_s.at[p, 2], ref.x_r.at[h, p, 2], {"feat": two}
            )
        for p, base, i, k1, k2, one, two in plans:
            copies.arrived(
                zf.at[i, at(base + k1 * half + (1 - k2) * quarter, quarter, 16)],
                ref.x_s.at[p, 2], ref.x_r.at[h, p, 2], {"feat": two},
            )
            mine = at(base + k1 * half, half, 16)
            copies.put(
                zf.at[i, mine], zf.at[i, mine], ref.x_s.at[p, 3], ref.x_r.at[h, p, 3], {"feat": one}
            )
        for p, base, i, k1, k2, one, two in plans:
            copies.arrived(
                zf.at[i, at(base + (1 - k1) * half, half, 16)],
                ref.x_s.at[p, 3], ref.x_r.at[h, p, 3], {"feat": one},
            )

    def gram_rows(zf, lefts):
        for n, left in enumerate(lefts):
            for i in range(2):
                ref.gs[n, :, i * 128 : i * 128 + 128] = jnp.dot(left, zf[i], preferred_element_type=F32)

    def gram_to_core(h, ng, copies):
        for d in range(1, nc):
            peer = after(c, d, nc)
            copies.put(
                ref.gs.at[0:ng, at(peer * 32, 32, 8)], ref.rgc.at[h, d - 1, 0:ng],
                ref.gc_s.at[d - 1], ref.gc_r.at[h, d - 1], {"tok_2": peer},
            )

    def gram_to_y(h, ng, copies):
        value = ref.gs[0:ng, at(c * 32, 32, 8), :]
        for d in range(1, nc):
            copies.arrived(
                ref.rgc.at[h, d - 1, 0:ng], ref.gc_s.at[d - 1], ref.gc_r.at[h, d - 1],
                {"tok_2": before(c, d, nc)},
            )
            value = value + ref.rgc[h, d - 1, 0:ng]
        ref.gy[0:ng] = value
        for d in range(1, ny):
            peer = after(y, d, ny)
            copies.put(
                ref.gy.at[0:ng, at(peer * 8, 8, 8)], ref.rgy.at[h, d - 1, 0:ng],
                ref.gy_s.at[d - 1], ref.gy_r.at[h, d - 1], {"tok_0": peer},
            )

    def gram_to_z(h, ng, copies):
        value = ref.gy[0:ng, at(y * 8, 8, 8), :]
        for d in range(1, ny):
            copies.arrived(
                ref.rgy.at[h, d - 1, 0:ng], ref.gy_s.at[d - 1], ref.gy_r.at[h, d - 1],
                {"tok_0": before(y, d, ny)},
            )
            value = value + ref.rgy[h, d - 1, 0:ng]
        ref.gz[0:ng] = value
        for d in range(1, nz):
            copies.put(
                ref.gz.at[0:ng], ref.rgz.at[h, d - 1, 0:ng],
                ref.gz_s.at[d - 1], ref.gz_r.at[h, d - 1], {"tok_1": after(z, d, nz)},
            )

    def gram_to_all(h, ng, copies):
        value = ref.gz[0:ng]
        for d in range(1, nz):
            copies.arrived(
                ref.rgz.at[h, d - 1, 0:ng], ref.gz_s.at[d - 1], ref.gz_r.at[h, d - 1],
                {"tok_1": before(z, d, nz)},
            )
            value = value + ref.rgz[h, d - 1, 0:ng]
        mine = place(x, y, c)
        ref.gm[0:ng] = value
        ref.ga[h, mine, 0:ng] = value
        for i, d in enumerate(plane):
            copies.put(
                ref.gm.at[0:ng], ref.ga.at[h, mine, 0:ng],
                ref.ga_s.at[i], ref.ga_r.at[h, i], on_plane(*d)[1],
            )

    def gram_whole(h, ng, copies):
        for i, (dx, dy, dc) in enumerate(plane):
            where, device = on_plane(-dx, -dy, -dc)
            copies.arrived(
                ref.ga.at[h, place(*where), 0:ng], ref.ga_s.at[i], ref.ga_r.at[h, i], device
            )
        for g in range(nx * ny * nc):
            for n in range(ng):
                ref.gram[n, g * 8 : g * 8 + 8, :] = ref.ga[h, g, n]

    def half_step(h, carry):
        copies = Copies()
        side = lax.rem(h, 2)
        source, target = ref.acts.at[1 - side], ref.acts.at[side]
        zf = ref.z.at[h]
        opening = h == 0

        @pl.when(opening)
        def _():
            loads[0].wait()
            loads[1].wait()

        def beside():
            @pl.when(opening)
            def _():
                loads[2].wait()
                column_sums()

        projected(h, source, zf, copies, opening, beside)
        for i in range(2):
            ref.zt[i * 128 : i * 128 + 128, :] = zf[i].T
        gram_rows(zf, [ref.zt[at(x * 64, 64, 16), :]])
        gram_to_core(h, 1, copies)
        for lo in range(0, feats, 256):
            hi = min(lo + 256, feats)
            ref.cb[lo:hi, :] = jnp.dot(ref.zt[...], target[:, lo:hi], preferred_element_type=F32).T
        for d in range(1, nc):
            peer = after(c, d, nc)
            rows = at(peer * per_c, per_c, PIECE)
            copies.put(
                ref.cb.at[rows], ref.rcc.at[h, d - 1],
                ref.cc_s.at[d - 1], ref.cc_r.at[h, d - 1], {"tok_2": peer},
            )
            copies.put(
                ref.sb.at[rows], ref.rsc.at[d - 1],
                ref.sc_s.at[d - 1], ref.sc_r.at[d - 1], {"tok_2": peer}, opening,
            )
        gram_to_y(h, 1, copies)

        own = at(c * per_c, per_c, PIECE)
        value = ref.cb[own, :]
        for d in range(1, nc):
            copies.arrived(
                ref.rcc.at[h, d - 1], ref.cc_s.at[d - 1], ref.cc_r.at[h, d - 1],
                {"tok_2": before(c, d, nc)},
            )
            value = value + ref.rcc[h, d - 1]
        ref.cy[...] = value
        for d in range(1, ny):
            peer = after(y, d, ny)
            copies.put(
                ref.cy.at[at(peer * per_y, per_y, PIECE)], ref.rcy.at[h, d - 1],
                ref.cy_s.at[d - 1], ref.cy_r.at[h, d - 1], {"tok_0": peer},
            )

        @pl.when(opening)
        def _():
            sums = ref.sb[own, :]
            for d in range(1, nc):
                copies.arrived(
                    ref.rsc.at[d - 1], ref.sc_s.at[d - 1], ref.sc_r.at[d - 1],
                    {"tok_2": before(c, d, nc)},
                )
                sums = sums + ref.rsc[d - 1]
            ref.sy[...] = sums

        for d in range(1, ny):
            peer = after(y, d, ny)
            copies.put(
                ref.sy.at[at(peer * per_y, per_y, PIECE)], ref.rsy.at[d - 1],
                ref.sy_s.at[d - 1], ref.sy_r.at[d - 1], {"tok_0": peer}, opening,
            )
        gram_to_z(h, 1, copies)
        own = at(y * per_y, per_y, PIECE)
        value = ref.cy[own, :]
        for d in range(1, ny):
            copies.arrived(
                ref.rcy.at[h, d - 1], ref.cy_s.at[d - 1], ref.cy_r.at[h, d - 1],
                {"tok_0": before(y, d, ny)},
            )
            value = value + ref.rcy[h, d - 1]
        ref.cz[...] = value

        def to_owner(peer):
            return at(lax.rem(peer, owners) * PIECE, PIECE, PIECE)

        for d in range(1, nz):
            peer = after(z, d, nz)
            copies.put(
                ref.cz.at[to_owner(peer)], ref.rcz.at[h, d - 1],
                ref.cz_s.at[d - 1], ref.cz_r.at[h, d - 1], {"tok_1": peer}, peer < owners,
            )

        @pl.when(opening)
        def _():
            sums = ref.sy[own, :]
            for d in range(1, ny):
                copies.arrived(
                    ref.rsy.at[d - 1], ref.sy_s.at[d - 1], ref.sy_r.at[d - 1],
                    {"tok_0": before(y, d, ny)},
                )
                sums = sums + ref.rsy[d - 1]
            ref.sz[...] = sums

        for d in range(1, nz):
            peer = after(z, d, nz)
            copies.put(
                ref.sz.at[to_owner(peer)], ref.rsz.at[d - 1],
                ref.sz_s.at[d - 1], ref.sz_r.at[d - 1], {"tok_1": peer}, opening & (peer < owners),
            )
        gram_to_all(h, 1, copies)

        owner = z < owners
        wf = ref.wf.at[h]
        row = c * per_c + y * per_y
        mine = at(row + lax.rem(z, owners) * PIECE, PIECE, PIECE)

        @pl.when(opening & owner)
        def _():
            sums = ref.sz[to_owner(z), :]
            for d in range(1, nz):
                copies.arrived(
                    ref.rsz.at[d - 1], ref.sz_s.at[d - 1], ref.sz_r.at[d - 1],
                    {"tok_1": before(z, d, nz)},
                )
                sums = sums + ref.rsz[d - 1]
            ref.ss[...] = sums

        @pl.when(owner)
        def _():
            value = ref.cz[to_owner(z), :]
            for d in range(1, nz):
                copies.arrived(
                    ref.rcz.at[h, d - 1], ref.cz_s.at[d - 1], ref.cz_r.at[h, d - 1],
                    {"tok_1": before(z, d, nz)},
                )
                value = value + ref.rcz[h, d - 1]
            sums = jnp.where(side == 0, ref.ss[:, 0:1], ref.ss[:, 64:65])
            value = (value * count) * (root / (sums * count + 0.5))
            ref.pc[...] = value
            wf[mine, :] = value

        for d in range(1, nz):
            copies.put(
                ref.pc, wf.at[mine], ref.wz_s.at[d - 1], ref.wz_r.at[h, d - 1],
                {"tok_1": after(z, d, nz)}, owner,
            )
        for d in range(1, nz):
            sender = before(z, d, nz)
            copies.arrived(
                wf.at[at(row + lax.rem(sender, owners) * PIECE, PIECE, PIECE)],
                ref.wz_s.at[d - 1], ref.wz_r.at[h, d - 1], {"tok_1": sender}, sender < owners,
            )
        for d in range(1, ny):
            mine = at(row, per_y, PIECE)
            copies.put(
                wf.at[mine], wf.at[mine], ref.wy_s.at[d - 1], ref.wy_r.at[h, d - 1],
                {"tok_0": after(y, d, ny)},
            )
        gram_whole(h, 1, copies)

        def between():
            for d in range(1, ny):
                sender = before(y, d, ny)
                copies.arrived(
                    wf.at[at(c * per_c + sender * per_y, per_y, PIECE)],
                    ref.wy_s.at[d - 1], ref.wy_r.at[h, d - 1], {"tok_0": sender},
                )
            for d in range(1, nc):
                mine = at(c * per_c, per_c, PIECE)
                copies.put(
                    wf.at[mine], wf.at[mine], ref.wc_s.at[d - 1], ref.wc_r.at[h, d - 1],
                    {"tok_2": after(c, d, nc)},
                )

        inverse_into(ref.gram.at[0], count, ref.inv, between)
        for d in range(1, nc):
            sender = before(c, d, nc)
            copies.arrived(
                wf.at[at(sender * per_c, per_c, PIECE)],
                ref.wc_s.at[d - 1], ref.wc_r.at[h, d - 1], {"tok_2": sender},
            )
        high_inv, low_inv = split(ref.inv[...])
        for lo in range(0, feats, feats // 4):
            rows = slice(lo, lo + feats // 4)
            high_w, low_w = split(wf[rows, :])
            value = mm(high_w, low_inv, 1, 1, None) + mm(low_w, high_inv, 1, 1, None)
            ref.w[rows, :] = (value + mm(high_w, high_inv, 1, 1, None)).astype(BF16)

        @pl.when(h == STEPS - 2)
        def _():
            ref.first_dirs[...] = ref.w[...]

        @pl.when(h == STEPS - 1)
        def _():
            ref.second_dirs[...] = ref.w[...]

        copies.drain()
        return carry

    lax.fori_loop(0, STEPS, half_step, 0)

    h = STEPS
    copies = Copies()
    zf = ref.z.at[h]
    projected(h, ref.acts.at[1], zf, copies, None, lambda: None)
    before_rows = ref.zt[at(x * 64, 64, 16), :]
    for i in range(2):
        ref.zl[i * 128 : i * 128 + 128, :] = zf[i].T
    gram_rows(zf, [ref.zl[at(x * 64, 64, 16), :], before_rows])
    gram_to_core(h, 2, copies)
    gram_to_y(h, 2, copies)
    gram_to_z(h, 2, copies)
    gram_to_all(h, 2, copies)
    gram_whole(h, 2, copies)
    left = mm(ref.inv[...], ref.gram[1] * count)
    inverse_into(ref.gram.at[0], count, ref.last)
    ref.correlation[...] = mm(left, ref.last[...], 1, 1)
    copies.drain()


def body(first_acts, second_acts, start_dirs):
    nx, ny, nz, nc = (lax.axis_size(a) for a in ("feat", *TOK))
    tokens, feats = first_acts.shape
    k = start_dirs.shape[1]
    per_y = (nz - 1) * PIECE
    per_c = ny * per_y
    assert per_c * nc == feats and nx == 4 and k == 256 and ny * nc == 8
    total = float(tokens * ny * nz * nc)
    root = float(feats * nx) ** 0.5
    vmem, hbm = pl.BlockSpec(memory_space=pltpu.VMEM), pl.BlockSpec(memory_space=pl.ANY)
    chunk = tokens // CHUNKS
    every = STEPS + 1
    parts = 2 * CHUNKS
    members = nx * ny * nc

    def f32(*shape):
        return pltpu.VMEM(shape, F32)

    def bf16(*shape):
        return pltpu.VMEM(shape, BF16)

    def dma(*shape):
        return pltpu.SemaphoreType.DMA(shape)

    ins = ["first_acts", "second_acts", "start_dirs"]
    outs = dict(
        first_dirs=jax.ShapeDtypeStruct((feats, k), BF16),
        second_dirs=jax.ShapeDtypeStruct((feats, k), BF16),
        correlation=jax.ShapeDtypeStruct((k, k), F32),
    )
    scratch = dict(
        acts=bf16(2, tokens, feats), load_sem=dma(3), w=bf16(feats, k),
        part=f32(tokens, k), out=bf16(2, tokens, 128), z=bf16(every, 2, tokens, 128),
        zt=bf16(k, tokens), zl=bf16(k, tokens),
        r1=bf16(every, parts, chunk // 2, 128), g2=bf16(parts, chunk // 4, 128),
        r2=bf16(every, parts, chunk // 4, 128), x_s=dma(parts, 4), x_r=dma(every, parts, 4),
        gs=f32(2, 64, k), rgc=f32(every, nc - 1, 2, 32, k), gc_s=dma(nc - 1), gc_r=dma(every, nc - 1),
        gy=f32(2, 32, k), rgy=f32(every, ny - 1, 2, 8, k), gy_s=dma(ny - 1), gy_r=dma(every, ny - 1),
        gz=f32(2, 8, k), rgz=f32(every, nz - 1, 2, 8, k), gz_s=dma(nz - 1), gz_r=dma(every, nz - 1),
        gm=f32(2, 8, k), ga=f32(every, members, 2, 8, k), ga_s=dma(members - 1),
        ga_r=dma(every, members - 1), gram=f32(2, k, k), inv=f32(k, k), last=f32(k, k),
        cb=f32(feats, k), rcc=f32(STEPS, nc - 1, per_c, k), cc_s=dma(nc - 1), cc_r=dma(STEPS, nc - 1),
        cy=f32(per_c, k), rcy=f32(STEPS, ny - 1, per_y, k), cy_s=dma(ny - 1), cy_r=dma(STEPS, ny - 1),
        cz=f32(per_y, k), rcz=f32(STEPS, nz - 1, PIECE, k), cz_s=dma(nz - 1), cz_r=dma(STEPS, nz - 1),
        sb=f32(feats, 128), rsc=f32(nc - 1, per_c, 128), sc_s=dma(nc - 1), sc_r=dma(nc - 1),
        sy=f32(per_c, 128), rsy=f32(ny - 1, per_y, 128), sy_s=dma(ny - 1), sy_r=dma(ny - 1),
        sz=f32(per_y, 128), rsz=f32(nz - 1, PIECE, 128), sz_s=dma(nz - 1), sz_r=dma(nz - 1),
        ss=f32(PIECE, 128), pc=f32(PIECE, k), wf=f32(STEPS, feats, k),
        wz_s=dma(nz - 1), wz_r=dma(STEPS, nz - 1), wy_s=dma(ny - 1), wy_r=dma(STEPS, ny - 1),
        wc_s=dma(nc - 1), wc_r=dma(STEPS, nc - 1),
    )
    names = [*ins, *outs, *scratch]
    return pl.pallas_call(
        functools.partial(kernel, names, total, root),
        out_shape=tuple(outs.values()),
        in_specs=[hbm, hbm, hbm],
        out_specs=(vmem, vmem, vmem),
        scratch_shapes=list(scratch.values()),
        compiler_params=pltpu.CompilerParams(
            collective_id=0, has_side_effects=True, vmem_limit_bytes=60 << 20
        ),
        name="cca",
    )(first_acts, second_acts, start_dirs)


def solution(mesh):
    split_mesh = Mesh(
        mesh.devices.reshape(4, 8, 2, mesh.shape["feat"]), ("tok_0", "tok_1", "tok_2", "feat")
    )
    in_specs = (P(TOK, "feat"), P(TOK, "feat"), P("feat", None))
    out_specs = (P("feat", None), P("feat", None), P())
    return jax.shard_map(
        body, mesh=split_mesh, in_specs=in_specs, out_specs=out_specs, check_vma=False
    )
```

time: 1000 us -> 269 us (0.27)
  other arithmetic: 291 us -> 0 us
  Pallas kernels: 0 us -> 263 us
  blocking collectives: 194 us -> 0 us
  waiting for transfers between devices: 182 us -> 0 us
  starting transfers between devices: 171 us -> 0 us
  local copies, waits for them, and re-layouts: 89.9 us -> 5.3 us
  matrix products: 52.5 us -> 0 us
    another operation x46 -> x0, other arithmetic: 276 us -> none  [the longest x27 139 us: half_step(): lower = jnp.linalg.cholesky(sums[0] / tokens)]
    pallas_call x0 -> x1, Pallas kernels: none -> 263 us  [body(): pl.pallas_call(functools.partial(kernel, names, total, root), out_shape=t...]
    all_to_all x22 -> x0, waiting for transfers between devices: 182 us -> none  [the longest x11 70.8 us: copy_for_each(): return lax.all_to_all(copies, axis, split_axis=0, concat_axis=0, tiled=True)]
    all_to_all x22 -> x0, starting transfers between devices: 171 us -> none  [the longest x11 77.8 us: copy_for_each(): return lax.all_to_all(copies, axis, split_axis=0, concat_axis=0, tiled=True)]
    psum x5 -> x0, blocking collectives: 147 us -> none  [project(): z_rows = lax.psum(partial_value, 'feat').astype(jnp.bfloat16)]
    all_to_all x7 -> x0, blocking collectives: 47.1 us -> none  [the longest x3 27.4 us: summed_on_arrival(): lax.all_to_all(blocks, axis, split_axis=0, concat_axis=0, tiled=True)]
    another operation x28 -> x0, matrix products: 29.6 us -> none  [the longest x12 17.1 us: half_step(): lax.linalg.triangular_solve(lower, cross, left_side=False, lower=True, tr...]
    another operation x53 -> x0, local copies, waits for them, and re-layouts: 27.6 us -> none  [the longest x30 17.7 us: half_step(): lax.linalg.triangular_solve(lower, cross, left_side=False, lower=True, tr...]
  transfers between devices with their start and end apart: 22 -> 0, of which waited for: 17 -> 0; matrix products, arithmetic and copies ran while one was open for 35% -> 0% of each run, Pallas kernels for 0% -> 0%
where the time goes in v2:
time: 269 us
  Pallas kernels  263 us (98%)
  local copies, waits for them, and re-layouts  5.3 us (2%)
    pallas_call x1, Pallas kernels, body(): pl.pallas_call(functools.partial(kernel, names, total, root), out_shape=t...  263 us

profile of v2, /device:TPU:1, one launch (start us, length us, event | category | flops | bytes accessed | tf_op | source)
XLA Modules:
  0.0 268.9 jit_solution(13322165949478528308)
XLA Ops:
  0.6 263.0 %cca.1 = (bf16[896,256]{1,0:T(8,128)(2,1)}, bf16[896,256]{1,0:T(8,128)(2,1)}, f32[256,256]{1,0:T(8,128)}) custom-call(bf16[1280,896]{1,0:T(8,128)(2,1)} %refs_0_.1, bf16[1280,896]{1,0:T(8,128)(2,1)} %refs_1_.1, bf16[896,256]{1,0:T(8,128)(2,1)} %refs_2_.1), custom_call_target="tpu_custom_call" | custom-call | tf_op jit(solution)/shard_map/cca/pallas_call | solution.py:574
  263.6 1.8 copy.9
  265.4 1.8 copy.10
  267.3 1.7 copy.11
